TPU v7x, 32 devices: a whole 2x2x4 slice. The times are simulated.
32 devices in a mesh: fsdp: 8 (over y, x, core), tp: 4 (over z).
Axes of the slice: x: 2, y: 2, z: 4, core: 2. Of those that a mesh axis runs over, the one named last changes fastest.
Arguments:
- inputs: bfloat16 [16, 1024, 1536], P('fsdp', 'tp'), may hold values from -6 to 6
- teacher: bfloat16 [16, 1024, 1536], P('fsdp', 'tp'), may hold values from -6 to 6
- seq_lengths: int32 [16], P('fsdp'), may hold values from 256 to 1024, as said below
- first_gain: float32 [1536], replicated, may hold values from 0.5 to 1.5
- branch_weight: bfloat16 [1536, 2048], P('fsdp', 'tp'), may hold values from -0.15625 to 0.15625
- branch_bias: float32 [2048], P('tp'), may hold values from -3 to 3
- gate_weight: bfloat16 [1536, 2048], P('fsdp', 'tp'), may hold values from -0.15625 to 0.15625
- gate_bias: float32 [2048], P('tp'), may hold values from -3 to 3
- conv_weight: float32 [4, 2048], P(None, 'tp'), may hold values from -3 to 3
- conv_bias: float32 [2048], P('tp'), may hold values from -2 to 2
- rate_weight: bfloat16 [8, 256, 256], P('tp', 'fsdp'), may hold values from -0.375 to 0.375
- rate_bias: float32 [2048], P('tp'), may hold values from -4 to 4
- inlet_weight: bfloat16 [8, 256, 256], P('tp', 'fsdp'), may hold values from -0.375 to 0.375
- inlet_bias: float32 [2048], P('tp'), may hold values from -4 to 4
- decay_param: float32 [2048], P('tp'), may hold values from 3 to 11
- out_weight: bfloat16 [2048, 1536], P('tp', 'fsdp'), may hold values from -0.375 to 0.375
- second_gain: float32 [1536], replicated, may hold values from 0.5 to 1.5
- geglu_gate: bfloat16 [1536, 4608], P('fsdp', 'tp'), may hold values from -0.15625 to 0.15625
- geglu_up: bfloat16 [1536, 4608], P('fsdp', 'tp'), may hold values from -0.15625 to 0.15625
- geglu_down: bfloat16 [4608, 1536], P('tp', 'fsdp'), may hold values from -0.125 to 0.125
Outputs:
- block_out: bfloat16 [16, 1024, 1536], P('fsdp', 'tp')
- loss_value: float32 [], replicated
- input_grad: float32 [16, 1024, 1536], P('fsdp', 'tp')
- first_gain_grad: float32 [1536], replicated
- branch_weight_grad: float32 [1536, 2048], P('fsdp', 'tp')
- branch_bias_grad: float32 [2048], P('tp')
- gate_weight_grad: float32 [1536, 2048], P('fsdp', 'tp')
- gate_bias_grad: float32 [2048], P('tp')
- conv_weight_grad: float32 [4, 2048], P(None, 'tp')
- conv_bias_grad: float32 [2048], P('tp')
- rate_weight_grad: float32 [8, 256, 256], P('tp', 'fsdp')
- rate_bias_grad: float32 [2048], P('tp')
- inlet_weight_grad: float32 [8, 256, 256], P('tp', 'fsdp')
- inlet_bias_grad: float32 [2048], P('tp')
- decay_param_grad: float32 [2048], P('tp')
- out_weight_grad: float32 [2048, 1536], P('tp', 'fsdp')
- second_gain_grad: float32 [1536], replicated
- geglu_gate_grad: float32 [1536, 4608], P('fsdp', 'tp')
- geglu_up_grad: float32 [1536, 4608], P('fsdp', 'tp')
- geglu_down_grad: float32 [4608, 1536], P('tp', 'fsdp')
Inputs may be any that keep to these rules, and one draw needn't show every extreme that they name: Position p of sequence s is valid where p < seq_lengths[s]; positions from seq_lengths[s] to 1023 are padding.
All inputs are finite; a program needn't handle non-finite values.
Results may differ from a plain program's by a relative error of at most 0.006.
Values may be sent and summed in bfloat16 or wider, within the bound.
No kernel may reach another device: no remote copies, remote signals or barrier semaphores. Data moves between devices by JAX's collectives and lax.ppermute only.
A program may use at most 256 MiB of HBM per device.

v0:
```python
import jax
import jax.numpy as jnp
from jax import lax
from jax.sharding import PartitionSpec as P

EPS = 1e-06
DECAY_SCALE = 8.0


def gather_rows(values):
    return lax.all_gather(values, "tp", axis=1, tiled=True)


def reduce_rows(make_term, full_len):
    return lax.psum_scatter(make_term(0, full_len), "tp", scatter_dimension=1, tiled=True)


def rms_norm(values, gain_vec):
    inv_rms = lax.rsqrt(jnp.mean(values * values, axis=-1, keepdims=True) + EPS)
    return values * inv_rms * gain_vec


def causal_conv(branch, kernel, offset_bias):
    tap_count = kernel.shape[0]
    seq_len = branch.shape[1]
    padded = jnp.pad(branch, ((0, 0), (tap_count - 1, 0), (0, 0)))
    running = jnp.zeros_like(branch) + offset_bias
    for tap_index in range(tap_count):
        begin = tap_count - 1 - tap_index
        running = running + kernel[tap_index] * padded[:, begin : begin + seq_len]
    return running


def linear_scan(decay_rate, source):

    def combine(earlier, later):
        return (earlier[0] * later[0], later[0] * earlier[1] + later[1])

    return lax.associative_scan(combine, (decay_rate, source), axis=1)[1]


def lru_gates(rate_pre, inlet_pre, decay_param, conv_out):
    rate_gate = jax.nn.sigmoid(rate_pre)
    inlet_gate = jax.nn.sigmoid(inlet_pre)
    log_decay = -DECAY_SCALE * rate_gate * jax.nn.softplus(-decay_param)
    decay_rate = jnp.exp(log_decay)
    normaliser = jnp.sqrt(-jnp.expm1(2.0 * log_decay))
    return (decay_rate, normaliser * inlet_gate * conv_out)


def dense(values, matrix):
    return jnp.einsum("slk,kn->sln", values, matrix, preferred_element_type=jnp.float32)


def dense_back(cotangent, matrix):
    return jnp.einsum("sln,kn->slk", cotangent, matrix, preferred_element_type=jnp.float32)


def outer_sum(values, cotangent):
    return jnp.einsum("slk,sln->kn", values, cotangent, preferred_element_type=jnp.float32)


def split_blocks(values, count_blocks):
    seqs_here, seq_len, channels = values.shape
    return values.reshape(seqs_here, seq_len, count_blocks, channels // count_blocks)


def shards(
    inputs,
    teacher,
    seq_lengths,
    first_gain,
    branch_weight,
    branch_bias,
    gate_weight,
    gate_bias,
    conv_weight,
    conv_bias,
    rate_weight,
    rate_bias,
    inlet_weight,
    inlet_bias,
    decay_param,
    out_weight,
    second_gain,
    geglu_gate,
    geglu_up,
    geglu_down,
):
    seq_dev, local_len, model_width = inputs.shape
    full_len = local_len * lax.axis_size("tp")
    count_blocks = rate_weight.shape[0]
    channels = branch_weight.shape[1]
    valid_total = lax.psum(jnp.sum(seq_lengths.astype(jnp.float32)), "fsdp")
    gathered = (
        lax.all_gather(branch_weight, "fsdp", axis=0, tiled=True),
        lax.all_gather(gate_weight, "fsdp", axis=0, tiled=True),
        lax.all_gather(rate_weight, "fsdp", axis=1, tiled=True),
        lax.all_gather(inlet_weight, "fsdp", axis=1, tiled=True),
        lax.all_gather(out_weight, "fsdp", axis=1, tiled=True),
        lax.all_gather(geglu_gate, "fsdp", axis=0, tiled=True),
        lax.all_gather(geglu_up, "fsdp", axis=0, tiled=True),
        lax.all_gather(geglu_down, "fsdp", axis=1, tiled=True),
    )
    w_branch, w_gate, w_rate, w_inlet, w_out, w_ffgate, w_ffup, w_ffdown = gathered
    residual = inputs.astype(jnp.float32)
    first_f, first_back = jax.vjp(rms_norm, residual, first_gain)
    first_rows = gather_rows(first_f.astype(jnp.bfloat16))
    branch_pre = dense(first_rows, w_branch) + branch_bias
    gate_pre = dense(first_rows, w_gate) + gate_bias
    gate_act, gate_back = jax.vjp(jax.nn.gelu, gate_pre)
    conv_raw, conv_back = jax.vjp(causal_conv, branch_pre, conv_weight, conv_bias)
    conv_out = conv_raw.astype(jnp.bfloat16)
    conv_split = split_blocks(conv_out, count_blocks)
    rate_pre = (
        jnp.einsum(
            "slbi,bij->slbj", conv_split, w_rate, preferred_element_type=jnp.float32
        ).reshape(seq_dev, full_len, channels)
        + rate_bias
    )
    inlet_pre = (
        jnp.einsum(
            "slbi,bij->slbj", conv_split, w_inlet, preferred_element_type=jnp.float32
        ).reshape(seq_dev, full_len, channels)
        + inlet_bias
    )
    (decay_rate, source), gates_back = jax.vjp(
        lru_gates, rate_pre, inlet_pre, decay_param, conv_out.astype(jnp.float32)
    )
    state = linear_scan(decay_rate, source)
    mixed = (state * gate_act).astype(jnp.bfloat16)

    def mixed_term(start, count):
        return dense(mixed, w_out)

    middle = residual + reduce_rows(mixed_term, full_len)
    second_f, second_back = jax.vjp(rms_norm, middle, second_gain)
    second_rows = gather_rows(second_f.astype(jnp.bfloat16))
    ff_gate = dense(second_rows, w_ffgate)
    ff_up = dense(second_rows, w_ffup)
    ff_act, ff_back = jax.vjp(jax.nn.gelu, ff_gate)
    ff_hidden = (ff_act * ff_up).astype(jnp.bfloat16)

    def hidden_term(start, count):
        return dense(ff_hidden, w_ffdown)

    final = middle + reduce_rows(hidden_term, full_len)
    positions = lax.axis_index("tp") * local_len + jnp.arange(local_len, dtype=jnp.int32)
    valid_mask = (positions[None, :] < seq_lengths[:, None]).astype(jnp.float32)[..., None]
    teacher_f = teacher.astype(jnp.float32)
    mismatch = final - teacher_f
    loss_part = jnp.sum(valid_mask * mismatch * mismatch)
    scaling = seq_dev * lax.axis_size("fsdp") * full_len / valid_total
    out_cot = valid_mask * mismatch * scaling
    ff_cot = gather_rows(out_cot.astype(jnp.bfloat16))
    d_hidden = dense_back(ff_cot, w_ffdown)
    g_ffdown = outer_sum(ff_hidden, ff_cot)
    d_up = (d_hidden * ff_act).astype(jnp.bfloat16)
    d_ffgate = ff_back(d_hidden * ff_up)[0].astype(jnp.bfloat16)
    g_ffgate = outer_sum(second_rows, d_ffgate)
    g_ffup = outer_sum(second_rows, d_up)

    def second_term(start, count):
        return dense_back(d_ffgate, w_ffgate) + dense_back(d_up, w_ffup)

    d_second = reduce_rows(second_term, full_len)
    d_mid_norm, g_second = second_back(d_second)
    d_middle = out_cot + d_mid_norm
    mid_cot = gather_rows(d_middle.astype(jnp.bfloat16))
    d_mixed = dense_back(mid_cot, w_out)
    g_out = outer_sum(mixed, mid_cot)
    d_gate = gate_back(d_mixed * state)[0].astype(jnp.bfloat16)
    d_state = d_mixed * gate_act
    next_decay = jnp.concatenate([decay_rate[:, 1:], jnp.zeros_like(decay_rate[:, :1])], axis=1)
    carried = jnp.flip(linear_scan(jnp.flip(next_decay, 1), jnp.flip(d_state, 1)), 1)
    prev_state = jnp.concatenate([jnp.zeros_like(state[:, :1]), state[:, :-1]], axis=1)
    d_rate_f, d_inlet_f, g_decay, d_conv_direct = gates_back((carried * prev_state, carried))
    d_rate = d_rate_f.astype(jnp.bfloat16)
    d_inlet = d_inlet_f.astype(jnp.bfloat16)
    rate_split = split_blocks(d_rate, count_blocks)
    inlet_split = split_blocks(d_inlet, count_blocks)
    g_rate = jnp.einsum(
        "slbi,slbj->bij", conv_split, rate_split, preferred_element_type=jnp.float32
    )
    g_inlet = jnp.einsum(
        "slbi,slbj->bij", conv_split, inlet_split, preferred_element_type=jnp.float32
    )
    conv_from_gates = jnp.einsum(
        "slbj,bij->slbi", rate_split, w_rate, preferred_element_type=jnp.float32
    ) + jnp.einsum("slbj,bij->slbi", inlet_split, w_inlet, preferred_element_type=jnp.float32)
    d_conv = d_conv_direct + conv_from_gates.reshape(seq_dev, full_len, channels)
    d_branch_f, g_conv_w, g_conv_b = conv_back(d_conv)
    d_branch = d_branch_f.astype(jnp.bfloat16)
    g_branch = outer_sum(first_rows, d_branch)
    g_gate = outer_sum(first_rows, d_gate)

    def first_term(start, count):
        return dense_back(d_branch, w_branch) + dense_back(d_gate, w_gate)

    d_first = reduce_rows(first_term, full_len)
    d_in_norm, g_first = first_back(d_first)
    input_grad = d_middle + d_in_norm
    small = lax.psum(
        (
            jnp.sum(d_branch.astype(jnp.float32), axis=(0, 1)),
            jnp.sum(d_gate.astype(jnp.float32), axis=(0, 1)),
            g_conv_w,
            g_conv_b,
            jnp.sum(d_rate.astype(jnp.float32), axis=(0, 1)),
            jnp.sum(d_inlet.astype(jnp.float32), axis=(0, 1)),
            g_decay,
        ),
        "fsdp",
    )
    stats = lax.psum((loss_part, g_first, g_second), ("fsdp", "tp"))
    loss_value = stats[0] / (model_width * valid_total)
    sent = (
        lax.psum_scatter(g_branch, "fsdp", scatter_dimension=0, tiled=True),
        lax.psum_scatter(g_gate, "fsdp", scatter_dimension=0, tiled=True),
        lax.psum_scatter(g_rate, "fsdp", scatter_dimension=1, tiled=True),
        lax.psum_scatter(g_inlet, "fsdp", scatter_dimension=1, tiled=True),
        lax.psum_scatter(g_out, "fsdp", scatter_dimension=1, tiled=True),
        lax.psum_scatter(g_ffgate, "fsdp", scatter_dimension=0, tiled=True),
        lax.psum_scatter(g_ffup, "fsdp", scatter_dimension=0, tiled=True),
        lax.psum_scatter(g_ffdown, "fsdp", scatter_dimension=1, tiled=True),
    )
    return (
        final.astype(jnp.bfloat16),
        loss_value,
        input_grad,
        stats[1],
        sent[0],
        small[0],
        sent[1],
        small[1],
        small[2],
        small[3],
        sent[2],
        small[4],
        sent[3],
        small[5],
        small[6],
        sent[4],
        stats[2],
        sent[5],
        sent[6],
        sent[7],
    )


def solution(mesh):
    placed = (
        P("fsdp", "tp", None),
        P("fsdp", "tp", None),
        P("fsdp"),
        P(),
        P("fsdp", "tp"),
        P("tp"),
        P("fsdp", "tp"),
        P("tp"),
        P(None, "tp"),
        P("tp"),
        P("tp", "fsdp", None),
        P("tp"),
        P("tp", "fsdp", None),
        P("tp"),
        P("tp"),
        P("tp", "fsdp"),
        P(),
        P("fsdp", "tp"),
        P("fsdp", "tp"),
        P("tp", "fsdp"),
    )
    return jax.shard_map(
        shards,
        mesh=mesh,
        in_specs=placed,
        out_specs=(
            P("fsdp", "tp", None),
            P(),
            P("fsdp", "tp", None),
            P(),
            P("fsdp", "tp"),
            P("tp"),
            P("fsdp", "tp"),
            P("tp"),
            P(None, "tp"),
            P("tp"),
            P("tp", "fsdp", None),
            P("tp"),
            P("tp", "fsdp", None),
            P("tp"),
            P("tp"),
            P("tp", "fsdp"),
            P(),
            P("fsdp", "tp"),
            P("fsdp", "tp"),
            P("tp", "fsdp"),
        ),
        check_vma=False,
    )
```

profile of v0, /device:TPU:0, one launch (start us, length us, event | category | flops | bytes accessed | tf_op | source)
XLA Modules:
  0.0 2551.0 jit_solution(7661270025675743842)
XLA Ops:
  39.1 117.5 %all-gather.11.cloned.1.call-done = bf16[2,1024,1536]{2,1,0:T(8,128)(2,1)} async-done(((bf16[2,256,1536]{2,1,0:T(8,128)(2,1)}), bf16[2,1024,1536]{2,1,0:T(8,128)(2,1)}) %all-gather.11.cloned.1.call-update) | async-done | bytes 6291472 | tf_op jit(solution)/shard_map/all_gather | solution.py:11
  407.4 209.7 %reduce-scatter.13.cloned.1.call-done = f32[2,256,1536]{2,1,0:T(8,128)} async-done(((f32[2,1024,1536]{2,1,0:T(8,128)}), f32[2,256,1536]{2,1,0:T(8,128)}) %reduce-scatter.13.cloned.1.call-update) | async-done | bytes 3145744 | tf_op jit(solution)/shard_map/reduce_scatter | solution.py:15
  622.9 30.8 %all-gather.21.cloned.1.call-done = bf16[1536,1152]{1,0:T(8,128)(2,1)} async-done(((bf16[192,1152]{1,0:T(8,128)(2,1)}), bf16[1536,1152]{1,0:T(8,128)(2,1)}) %all-gather.21.cloned.1.call-update) | async-done | bytes 3538960 | tf_op jit(solution)/shard_map/all_gather | solution.py:101
  653.7 117.5 %all-gather.19.cloned.1.call-done = bf16[2,1024,1536]{2,1,0:T(8,128)(2,1)} async-done(((bf16[2,256,1536]{2,1,0:T(8,128)(2,1)}), bf16[2,1024,1536]{2,1,0:T(8,128)(2,1)}) %all-gather.19.cloned.1.call-update) | async-done | bytes 6291472 | tf_op jit(solution)/shard_map/all_gather | solution.py:11
  784.8 20.3 all-gather.23.cloned.1.call-done
  821.7 19.2 all-gather.25.cloned.1.call-done
  871.6 195.5 %reduce-scatter.15.cloned.1.call-done = f32[2,256,1536]{2,1,0:T(8,128)} async-done(((f32[2,1024,1536]{2,1,0:T(8,128)}), f32[2,256,1536]{2,1,0:T(8,128)}) %reduce-scatter.15.cloned.1.call-update) | async-done | bytes 3145744 | tf_op jit(solution)/shard_map/reduce_scatter | solution.py:15
  1071.2 116.5 %all-gather.27.cloned.1.call-done = bf16[2,1024,1536]{2,1,0:T(8,128)(2,1)} async-done(((bf16[2,256,1536]{2,1,0:T(8,128)(2,1)}), bf16[2,1024,1536]{2,1,0:T(8,128)(2,1)}) %all-gather.27.cloned.1.call-update) | async-done | bytes 6291472 | tf_op jit(solution)/shard_map/all_gather | solution.py:11
  1187.7 21.5 multiply_convert_fusion
  1236.3 210.0 %reduce-scatter.17.cloned.1.call-done = f32[2,256,1536]{2,1,0:T(8,128)} async-done(((f32[2,1024,1536]{2,1,0:T(8,128)}), f32[2,256,1536]{2,1,0:T(8,128)}) %reduce-scatter.17.cloned.1.call-update) | async-done | bytes 3145744 | tf_op jit(solution)/shard_map/reduce_scatter | solution.py:15
  1510.9 17.1 slice.596
  1545.1 26.8 %all-gather.29.cloned.1.call-done = bf16[2,1024,1536]{2,1,0:T(8,128)(2,1)} async-done(((bf16[2,256,1536]{2,1,0:T(8,128)(2,1)}), bf16[2,1024,1536]{2,1,0:T(8,128)(2,1)}) %all-gather.29.cloned.1.call-update) | async-done | bytes 6291472 | tf_op jit(solution)/shard_map/all_gather | solution.py:11
  1791.3 32.7 %rev.6 = f32[2,1024,512]{2,1,0:T(8,128)} reverse(f32[2,1024,512]{2,1,0:T(8,128)} %add.537), dimensions={1} | reverse | bytes 8388608 | tf_op jit(solution)/shard_map/jit(_flip)/rev | solution.py:175
  1973.4 25.2 all-reduce.52
  1998.6 108.7 %reduce-scatter.19.cloned.1.call-done = f32[2,256,1536]{2,1,0:T(8,128)} async-done(((f32[2,1024,1536]{2,1,0:T(8,128)}), f32[2,256,1536]{2,1,0:T(8,128)}) %reduce-scatter.19.cloned.1.call-update) | async-done | bytes 3145744 | tf_op jit(solution)/shard_map/reduce_scatter | solution.py:15
  2110.1 42.3 %all-reduce.51 = (f32[]{:T(128)}, f32[1536]{0:T(1024)}, f32[1536]{0:T(1024)}) all-reduce(f32[]{:T(128)} %get-tuple-element.29, f32[1536]{0:T(1024)S(1)} %get-tuple-element.26, f32[1536]{0:T(1024)S(1)} %copy-done.50), channel_id=1, replica_groups=mesh['fsdp'=8,'tp'=4] {'fsdp','tp'}, use_global_device_ids=true, to_apply=%region_5.6 | all-reduce | flops 3073 | bytes 24584 | tf_op jit(solution)/shard_map/psum | solution.py:215
  2158.4 20.0 reduce-scatter.35.cloned.1.call-done
  2178.4 69.5 %reduce-scatter.33.cloned.1.call-done = f32[192,1152]{1,0:T(8,128)} async-done(((f32[1536,1152]{1,0:T(8,128)}), f32[192,1152]{1,0:T(8,128)}) %reduce-scatter.33.cloned.1.call-update) | async-done | bytes 884752 | tf_op jit(solution)/shard_map/reduce_scatter | solution.py:224
  2247.9 69.5 %reduce-scatter.31.cloned.1.call-done = f32[192,1152]{1,0:T(8,128)} async-done(((f32[1536,1152]{1,0:T(8,128)}), f32[192,1152]{1,0:T(8,128)}) %reduce-scatter.31.cloned.1.call-update) | async-done | bytes 884752 | tf_op jit(solution)/shard_map/reduce_scatter | solution.py:223
  2317.3 37.6 %reduce-scatter.27.cloned.1.call-done = f32[2,32,256]{2,1,0:T(8,128)} async-done(((f32[2,256,256]{2,1,0:T(8,128)}), f32[2,32,256]{2,1,0:T(8,128)}) %reduce-scatter.27.cloned.1.call-update) | async-done | bytes 65552 | tf_op jit(solution)/shard_map/reduce_scatter | solution.py:221
  2355.0 37.8 %reduce-scatter.25.cloned.1.call-done = f32[2,32,256]{2,1,0:T(8,128)} async-done(((f32[2,256,256]{2,1,0:T(8,128)}), f32[2,32,256]{2,1,0:T(8,128)}) %reduce-scatter.25.cloned.1.call-update) | async-done | bytes 65552 | tf_op jit(solution)/shard_map/reduce_scatter | solution.py:220
  2392.8 49.9 %reduce-scatter.29.cloned.1.call-done = f32[512,192]{0,1:T(8,128)} async-done(((f32[512,1536]{0,1:T(8,128)}), f32[512,192]{0,1:T(8,128)}) %reduce-scatter.29.cloned.1.call-update) | async-done | bytes 393232 | tf_op jit(solution)/shard_map/reduce_scatter | solution.py:222
  2442.7 50.0 %reduce-scatter.23.cloned.1.call-done = f32[192,512]{1,0:T(8,128)} async-done(((f32[1536,512]{1,0:T(8,128)}), f32[192,512]{1,0:T(8,128)}) %reduce-scatter.23.cloned.1.call-update) | async-done | bytes 393232 | tf_op jit(solution)/shard_map/reduce_scatter | solution.py:219
  2492.8 50.0 %reduce-scatter.21.cloned.1.call-done = f32[192,512]{1,0:T(8,128)} async-done(((f32[1536,512]{1,0:T(8,128)}), f32[192,512]{1,0:T(8,128)}) %reduce-scatter.21.cloned.1.call-update) | async-done | bytes 393232 | tf_op jit(solution)/shard_map/reduce_scatter | solution.py:218
  (505 shorter events, 836.1 us)
Async XLA Ops:
  7.2 31.9 %all-gather.13.cloned.1.call-start = ((), (), s32[]{:S(2)}) async-start(), calls=%async_computation.13 | async-start | bytes 1769472 | tf_op jit(solution)/shard_map/all_gather | solution.py:96
  8.0 148.6 %all-gather.11.cloned.1.call-start = ((), (), s32[]{:S(2)}) async-start(), calls=%async_computation.12 | async-start | bytes 7864320 | tf_op jit(solution)/shard_map/all_gather | solution.py:11
  12.8 371.5 %all-gather.15.cloned.1.call-start = ((), (), s32[]{:S(2)}) async-start(), calls=%async_computation.14 | async-start | bytes 1769472 | tf_op jit(solution)/shard_map/all_gather | solution.py:97
  13.6 384.7 %all-gather.17.cloned.1.call-start = ((), (), s32[]{:S(2)}) async-start(), calls=%async_computation.15 | async-start | bytes 1769472 | tf_op jit(solution)/shard_map/all_gather | solution.py:100
  14.2 602.9 %reduce-scatter.13.cloned.1.call-start = ((), (), s32[]{:S(2)}) async-start(), calls=%async_computation.16 | async-start | bytes 15728640 | tf_op jit(solution)/shard_map/reduce_scatter | solution.py:15
  14.2 192.8 %copy-start.51 = (f32[512]{0:T(512)}, f32[512]{0:T(512)S(1)}, u32[]{:S(2)}) copy-start(f32[512]{0:T(512)S(1)} %broadcast_multiply_fusion.4) | copy-start | bytes 6148
  406.7 213.1 %copy-start.36 = (f32[1536]{0:T(1024)S(1)}, f32[1536]{0:T(1024)}, u32[]{:S(2)}) copy-start(f32[1536]{0:T(1024)} %param.36) | copy-start | bytes 18436
  406.8 246.9 %all-gather.21.cloned.1.call-start = ((), (), s32[]{:S(2)}) async-start(), calls=%async_computation.18 | async-start | bytes 3981312 | tf_op jit(solution)/shard_map/all_gather | solution.py:101
  407.3 363.8 %all-gather.19.cloned.1.call-start = ((), (), s32[]{:S(2)}) async-start(), calls=%async_computation.17 | async-start | bytes 7864320 | tf_op jit(solution)/shard_map/all_gather | solution.py:11
  621.4 183.7 %all-gather.23.cloned.1.call-start = ((), (), s32[]{:S(2)}) async-start(), calls=%async_computation.19 | async-start | bytes 3981312 | tf_op jit(solution)/shard_map/all_gather | solution.py:102
  622.1 218.7 %all-gather.25.cloned.1.call-start = ((), (), s32[]{:S(2)}) async-start(), calls=%async_computation.20 | async-start | bytes 3981312 | tf_op jit(solution)/shard_map/all_gather | solution.py:103
  622.9 444.2 %reduce-scatter.15.cloned.1.call-start = ((), (), s32[]{:S(2)}) async-start(), calls=%async_computation.21 | async-start | bytes 15728640 | tf_op jit(solution)/shard_map/reduce_scatter | solution.py:15
  855.0 332.7 %all-gather.27.cloned.1.call-start = ((), (), s32[]{:S(2)}) async-start(), calls=%async_computation.22 | async-start | bytes 7864320 | tf_op jit(solution)/shard_map/all_gather | solution.py:11
  1071.2 375.1 %reduce-scatter.17.cloned.1.call-start = ((), (), s32[]{:S(2)}) async-start(), calls=%async_computation.23 | async-start | bytes 15728640 | tf_op jit(solution)/shard_map/reduce_scatter | solution.py:15
  1236.1 335.8 %all-gather.29.cloned.1.call-start = ((), (), s32[]{:S(2)}) async-start(), calls=%async_computation.24 | async-start | bytes 7864320 | tf_op jit(solution)/shard_map/all_gather | solution.py:11
  1455.4 651.9 %reduce-scatter.19.cloned.1.call-start = ((), (), s32[]{:S(2)}) async-start(), calls=%async_computation.25 | async-start | bytes 15728640 | tf_op jit(solution)/shard_map/reduce_scatter | solution.py:15
  1897.1 281.3 %reduce-scatter.35.cloned.1.call-start = ((), (), s32[]{:S(2)}) async-start(), calls=%async_computation.33 | async-start | bytes 7962624 | tf_op jit(solution)/shard_map/reduce_scatter | solution.py:225
  1911.0 336.9 %reduce-scatter.33.cloned.1.call-start = ((), (), s32[]{:S(2)}) async-start(), calls=%async_computation.32 | async-start | bytes 7962624 | tf_op jit(solution)/shard_map/reduce_scatter | solution.py:224
  1924.8 392.5 %reduce-scatter.31.cloned.1.call-start = ((), (), s32[]{:S(2)}) async-start(), calls=%async_computation.31 | async-start | bytes 7962624 | tf_op jit(solution)/shard_map/reduce_scatter | solution.py:223
  1938.8 416.2 %reduce-scatter.27.cloned.1.call-start = ((), (), s32[]{:S(2)}) async-start(), calls=%async_computation.29 | async-start | bytes 589824 | tf_op jit(solution)/shard_map/reduce_scatter | solution.py:221
  1943.5 449.3 %reduce-scatter.25.cloned.1.call-start = ((), (), s32[]{:S(2)}) async-start(), calls=%async_computation.28 | async-start | bytes 589824 | tf_op jit(solution)/shard_map/reduce_scatter | solution.py:220
  1946.8 495.9 %reduce-scatter.29.cloned.1.call-start = ((), (), s32[]{:S(2)}) async-start(), calls=%async_computation.30 | async-start | bytes 3538944 | tf_op jit(solution)/shard_map/reduce_scatter | solution.py:222
  1955.5 537.2 %reduce-scatter.23.cloned.1.call-start = ((), (), s32[]{:S(2)}) async-start(), calls=%async_computation.27 | async-start | bytes 3538944 | tf_op jit(solution)/shard_map/reduce_scatter | solution.py:219
  1963.7 579.1 %reduce-scatter.21.cloned.1.call-start = ((), (), s32[]{:S(2)}) async-start(), calls=%async_computation.26 | async-start | bytes 3538944 | tf_op jit(solution)/shard_map/reduce_scatter | solution.py:218
  (77 other events, 3091.3 us)
Sparse Core Ops, SparseCore 0:
  9.9 29.1 all-gather.12
  41.3 115.3 all-gather.10
  158.5 23.7 all-gather.14
  184.0 25.5 all-gather.16
  406.9 210.1 reduce-scatter.12
  618.8 34.8 all-gather.20
  655.8 115.3 all-gather.18
  773.1 32.0 all-gather.22
  807.0 33.8 all-gather.24
  855.1 211.8 reduce-scatter.14
  1071.3 116.3 all-gather.26
  1236.2 210.0 reduce-scatter.16
  1455.5 116.3 all-gather.28
  1897.2 210.0 reduce-scatter.18
  2111.2 67.1 reduce-scatter.34
  2182.4 65.4 reduce-scatter.32
  2251.8 65.4 reduce-scatter.30
  2320.9 34.0 reduce-scatter.26
  2358.6 34.1 reduce-scatter.24
  2396.6 46.0 reduce-scatter.28
  2446.7 46.0 reduce-scatter.22
  2496.7 46.0 reduce-scatter.20
where the time goes:
time: 2570 us; the launch traced here: 2550 us
  waiting for transfers between devices  1560 us (61%)
  local copies, waits for them, and re-layouts  472 us (18%)
  matrix products  227 us (9%)
  other arithmetic  163 us (6%)
  blocking collectives  103 us (4%)
    reduce_scatter x4, waiting for transfers between devices, reduce_rows(): lax.psum_scatter(make_term(0, full_len), 'tp', scatter_dimension=1, tiled...  724 us
    all_gather x4, waiting for transfers between devices, gather_rows(): return lax.all_gather(values, 'tp', axis=1, tiled=True)  378 us
    slice x126, local copies, waits for them, and re-layouts, linear_scan(): return lax.associative_scan(combine, (decay_rate, source), axis=1)[1]  326 us
    dot_general x6, matrix products, dense(): jnp.einsum('slk,kn->sln', values, matrix, preferred_element_type=jnp.floa...  73.1 us
    dot_general x6, matrix products, dense_back(): jnp.einsum('sln,kn->slk', cotangent, matrix, preferred_element_type=jnp.f...  71.9 us
    reduce_scatter x1, waiting for transfers between devices, shards(): lax.psum_scatter(g_ffup, 'fsdp', scatter_dimension=0, tiled=True)  69.5 us
    reduce_scatter x1, waiting for transfers between devices, shards(): lax.psum_scatter(g_ffgate, 'fsdp', scatter_dimension=0, tiled=True)  69.5 us
    dot_general x6, matrix products, outer_sum(): jnp.einsum('slk,sln->kn', values, cotangent, preferred_element_type=jnp.f...  66.8 us
  transfers between devices with their start and end apart: 22, of which 20 were waited for; matrix products, arithmetic and copies ran while one was open for 18% of the time, Pallas kernels for 0%

commit v1 on v0

v1 whole, which is shorter than its diff:
```python
import functools

import jax
import jax.numpy as jnp
from jax import lax
from jax.experimental import pallas as pl
from jax.experimental.pallas import tpu as pltpu
from jax.sharding import PartitionSpec as P

EPS = 1e-06
DECAY_SCALE = 8.0
BF = jnp.bfloat16
F32 = jnp.float32
STEP = 16
GELU_A = 0.7978845608028654
GELU_B = 0.044715


def swap(values, axis_name, bit):
    size = lax.axis_size(axis_name)
    return lax.ppermute(values, axis_name, [(i, i ^ bit) for i in range(size)])


def bits_of(count):
    return [1 << b for b in range(count.bit_length() - 1)]


def in_core_order(mine, other, core, axis):
    first = jnp.where(core == 0, mine, other)
    second = jnp.where(core == 0, other, mine)
    return jnp.concatenate([first, second], axis=axis)


def pick_half(values, which, axis):
    low, high = jnp.split(values, 2, axis=axis)
    return jnp.where(which == 0, low, high)


def xor_blocks(values, axis, count, index):
    blocks = jnp.split(values, count, axis=axis)
    for bit in bits_of(count):
        flipped = (index & bit) != 0
        blocks = [jnp.where(flipped, blocks[j ^ bit], blocks[j]) for j in range(count)]
    return jnp.concatenate(blocks, axis=axis)


def lane_blocks(values, count, wanted):
    width = values.shape[1] // count
    runs, start = [], 0
    while start < len(wanted):
        stop = start + 1
        while stop < len(wanted) and wanted[stop] == wanted[stop - 1] + 1:
            stop += 1
        runs.append(values[:, wanted[start] * width : (wanted[stop - 1] + 1) * width])
        start = stop
    return runs[0] if len(runs) == 1 else jnp.concatenate(runs, axis=1)


def gather_matrix(unit, order):
    held = [0]
    for kind, bit in order:
        other = swap(unit, *((("tp", bit)) if kind == "z" else ("fsdp", 2 * bit)))
        if kind == "z":
            unit = jnp.concatenate([unit, other], axis=0)
            continue
        width = unit.shape[1] // len(held)
        parts = {j: unit[:, k * width : (k + 1) * width] for k, j in enumerate(held)}
        parts |= {j ^ bit: other[:, k * width : (k + 1) * width] for k, j in enumerate(held)}
        held = sorted(parts)
        unit = jnp.concatenate([parts[j] for j in held], axis=1)
    return unit


def scatter_matrix(total, order, chips):
    held = list(range(chips))
    for step, (kind, bit) in enumerate(reversed(order)):
        if kind == "z":
            keep, send = jnp.split(total, 2, axis=0)
            got = swap(send, "tp", bit)
        else:
            at = {j: k for k, j in enumerate(held)}
            count = len(held)
            send = lane_blocks(total, count, [at[j] for j in held if j & bit])
            keep = lane_blocks(total, count, [at[j] for j in held if not j & bit])
            held = [j for j in held if not j & bit]
            got = swap(send, "fsdp", 2 * bit)
        total = keep.astype(F32) + got.astype(F32)
        if step < len(order) - 1:
            total = total.astype(BF)
    return total


def minus_expm1(y):
    series = 1.0 + y * (1.0 / 7.0)
    for n in (6.0, 5.0, 4.0, 3.0, 2.0):
        series = 1.0 + y * (1.0 / n) * series
    return jnp.where(y > -0.35, -y * series, 1.0 - jnp.exp(y))


def sigmoid(v):
    return 0.5 * jnp.tanh(0.5 * v) + 0.5


def rows_iota(width):
    return lax.broadcasted_iota(jnp.int32, (8, width), 0)


def forward_kernel(
    branch,
    halo,
    conv_w,
    vectors,
    rate_w,
    inlet_w,
    conv_out,
    decay_out,
    local_out,
    prod_out,
    ext,
    rate_s,
    inlet_s,
):
    length, width = branch.shape[1:]
    ext[0:8] = halo[0]
    ext[8:] = branch[0]
    taps = conv_w.shape[0]

    def conv_step(i, carry):
        at = pl.multiple_of(i * STEP, STEP)
        window = ext[pl.ds(at, STEP + 8), :]
        total = jnp.broadcast_to(vectors[0:1, :], (STEP, width))
        for k in range(taps):
            total = total + conv_w[k : k + 1, :] * window[8 - k : 8 - k + STEP]
        conv_out[0, pl.ds(at, STEP), :] = total.astype(BF)
        return carry

    lax.fori_loop(0, length // STEP, conv_step, 0)
    mixed = conv_out[0]
    rate_s[...] = jnp.dot(mixed, rate_w[0], preferred_element_type=F32) + vectors[1:2, :]
    inlet_s[...] = jnp.dot(mixed, inlet_w[0], preferred_element_type=F32) + vectors[2:3, :]
    row = rows_iota(width)

    def scan_step(i, carry):
        at = pl.multiple_of(i * STEP, STEP)
        rows = pl.ds(at, STEP)
        rate = sigmoid(rate_s[rows, :])
        log_decay = (-DECAY_SCALE * rate) * vectors[3:4, :]
        decay = jnp.exp(log_decay)
        scale = jnp.sqrt(minus_expm1(2.0 * log_decay))
        source = scale * sigmoid(inlet_s[rows, :]) * conv_out[0, rows, :].astype(F32)
        decay_out[0, rows, :] = decay
        held, prod = carry
        for part in range(STEP // 8):
            a = decay[8 * part : 8 * part + 8]
            b = source[8 * part : 8 * part + 8]
            for k in (1, 2, 4):
                ok = row >= k
                b = jnp.where(ok, a * pltpu.roll(b, k, 0) + b, b)
                a = jnp.where(ok, a * pltpu.roll(a, k, 0), a)
            b = b + a * held
            a = a * prod
            here = pl.ds(at + 8 * part, 8)
            local_out[0, here, :] = b
            prod_out[0, here, :] = a
            held, prod = b[7:8], a[7:8]
        return held, prod

    lax.fori_loop(
        0,
        length // STEP,
        scan_step,
        (jnp.zeros((1, width), F32), jnp.ones((1, width), F32)),
    )


def block_spec(shape, index):
    return pl.BlockSpec(shape, index)


def run_forward(branch, halo, conv_w, vectors, rate_w, inlet_w):
    seqs, length, channels = branch.shape
    width = rate_w.shape[1]
    wide = pl.BlockSpec((1, length, width), lambda j, s: (s, 0, j))
    gate = pl.BlockSpec((1, width, width), lambda j, s: (j, 0, 0))
    full = lambda dt: jax.ShapeDtypeStruct(branch.shape, dt)
    return pl.pallas_call(
        forward_kernel,
        grid=(channels // width, seqs),
        in_specs=[
            wide,
            pl.BlockSpec((1, 8, width), lambda j, s: (s, 0, j)),
            pl.BlockSpec((conv_w.shape[0], width), lambda j, s: (0, j)),
            pl.BlockSpec((vectors.shape[0], width), lambda j, s: (0, j)),
            gate,
            gate,
        ],
        out_specs=[wide] * 4,
        out_shape=[full(BF), full(F32), full(F32), full(F32)],
        scratch_shapes=[
            pltpu.VMEM((length + 8, width), F32),
            pltpu.VMEM((length, width), F32),
            pltpu.VMEM((length, width), F32),
        ],
        cost_estimate=pl.CostEstimate(
            flops=60 * branch.size + 4 * branch.size * width,
            bytes_accessed=20 * branch.size,
            transcendentals=4 * branch.size,
        ),
        name="forward_scan",
    )(branch, halo, conv_w, vectors, rate_w, inlet_w)


def gelu_parts(x):
    square = x * x
    t = jnp.tanh(GELU_A * x * (1.0 + GELU_B * square))
    half = 0.5 * (1.0 + t)
    slope = half + 0.5 * x * (1.0 - t * t) * (GELU_A * (1.0 + 3.0 * GELU_B * square))
    return x * half, slope


def backward_scan_kernel(d_mixed, gate_pre, state, decay, d_gate, local_out, prod_out):
    length, width = state.shape[1:]
    row = rows_iota(width)

    def step(n, carry):
        at = pl.multiple_of(length - STEP - n * STEP, STEP)
        rows = pl.ds(at, STEP)
        dm = d_mixed[0, rows, :].astype(F32)
        act, slope = gelu_parts(gate_pre[0, rows, :])
        d_gate[0, rows, :] = (dm * state[0, rows, :] * slope).astype(BF)
        d_state = dm * act
        all_decay = decay[0, rows, :]
        held, prod, above = carry
        for part in reversed(range(STEP // 8)):
            plain = all_decay[8 * part : 8 * part + 8]
            a = jnp.where(row == 7, above, pltpu.roll(plain, 7, 0))
            b = d_state[8 * part : 8 * part + 8]
            for k in (1, 2, 4):
                ok = row < 8 - k
                b = jnp.where(ok, a * pltpu.roll(b, 8 - k, 0) + b, b)
                a = jnp.where(ok, a * pltpu.roll(a, 8 - k, 0), a)
            b = b + a * held
            a = a * prod
            here = pl.ds(at + 8 * part, 8)
            local_out[0, here, :] = b
            prod_out[0, here, :] = a
            held, prod, above = b[0:1], a[0:1], plain[0:1]
        return held, prod, above

    one = jnp.ones((1, width), F32)
    lax.fori_loop(0, length // STEP, step, (jnp.zeros((1, width), F32), one, one))


def run_backward_scan(d_mixed, gate_pre, state, decay, width):
    seqs, length, channels = state.shape
    wide = pl.BlockSpec((1, length, width), lambda j, s: (s, 0, j))
    full = lambda dt: jax.ShapeDtypeStruct(state.shape, dt)
    return pl.pallas_call(
        backward_scan_kernel,
        grid=(channels // width, seqs),
        in_specs=[wide] * 4,
        out_specs=[wide] * 3,
        out_shape=[full(BF), full(F32), full(F32)],
        cost_estimate=pl.CostEstimate(
            flops=60 * state.size, bytes_accessed=24 * state.size, transcendentals=state.size
        ),
        name="backward_scan",
    )(d_mixed, gate_pre, state, decay)


def backward_gates_kernel(
    local_c,
    prod_c,
    carry_in,
    state,
    state_in,
    conv_out,
    branch,
    halo,
    conv_w,
    vectors,
    rate_w,
    inlet_w,
    d_branch,
    head_out,
    tail_out,
    g_rate,
    g_inlet,
    sums,
    branch_x,
    state_x,
    rate_s,
    inlet_s,
    d_rate_s,
    d_inlet_s,
    d_conv_x,
):
    length, width = state.shape[1:]
    taps = conv_w.shape[0]
    seq = pl.program_id(1)
    branch_x[0:8] = halo[0]
    branch_x[8:] = branch[0]
    state_x[0:8] = jnp.broadcast_to(state_in[0], (8, width))
    state_x[8:] = state[0]
    mixed = conv_out[0]
    rate_s[...] = jnp.dot(mixed, rate_w[0], preferred_element_type=F32) + vectors[1:2, :]
    inlet_s[...] = jnp.dot(mixed, inlet_w[0], preferred_element_type=F32) + vectors[2:3, :]
    zero = jnp.zeros((8, width), F32)

    @pl.when(seq == 0)
    def _():
        g_rate[...] = jnp.zeros_like(g_rate)
        g_inlet[...] = jnp.zeros_like(g_inlet)
        sums[...] = jnp.zeros_like(sums)

    def fold(v):
        total = v[0:8]
        for part in range(1, STEP // 8):
            total = total + v[8 * part : 8 * part + 8]
        return total

    def gate_step(i, carry):
        s_decay, s_rate, s_inlet = carry
        at = pl.multiple_of(i * STEP, STEP)
        rows = pl.ds(at, STEP)
        rate = sigmoid(rate_s[rows, :])
        inlet = sigmoid(inlet_s[rows, :])
        log_decay = (-DECAY_SCALE * rate) * vectors[3:4, :]
        decay = jnp.exp(log_decay)
        scale = jnp.sqrt(minus_expm1(2.0 * log_decay))
        conv = conv_out[0, rows, :].astype(F32)
        cot = local_c[0, rows, :] + prod_c[0, rows, :] * carry_in[0]
        before = state_x[pl.ds(at, STEP + 8), :][7 : 7 + STEP]
        gated = cot * inlet
        d_log = cot * before * decay - gated * conv * (decay * decay) / scale
        weighted = d_log * rate
        d_rate = (weighted * (1.0 - rate) * (-DECAY_SCALE * vectors[3:4, :])).astype(BF)
        d_inlet = (gated * scale * conv * (1.0 - inlet)).astype(BF)
        d_rate_s[rows, :] = d_rate
        d_inlet_s[rows, :] = d_inlet
        d_conv_x[rows, :] = gated * scale
        return (
            s_decay + fold(weighted),
            s_rate + fold(d_rate.astype(F32)),
            s_inlet + fold(d_inlet.astype(F32)),
        )

    s_decay, s_rate, s_inlet = lax.fori_loop(0, length // STEP, gate_step, (zero, zero, zero))
    d_rate, d_inlet = d_rate_s[...], d_inlet_s[...]
    over_rows = (((0,), (0,)), ((), ()))
    transposed = (((1,), (1,)), ((), ()))
    g_rate[0] += lax.dot_general(mixed, d_rate, over_rows, preferred_element_type=F32)
    g_inlet[0] += lax.dot_general(mixed, d_inlet, over_rows, preferred_element_type=F32)
    d_conv_x[0:length] += lax.dot_general(
        d_rate, rate_w[0], transposed, preferred_element_type=F32
    ) + lax.dot_general(d_inlet, inlet_w[0], transposed, preferred_element_type=F32)
    d_conv_x[length:] = zero
    head_out[0] = d_conv_x[0:8]

    def conv_step(i, carry):
        at = pl.multiple_of(i * STEP, STEP)
        ahead = d_conv_x[pl.ds(at, STEP + 8), :]
        behind = branch_x[pl.ds(at, STEP + 8), :]
        here = ahead[0:STEP]
        total = conv_w[0:1, :] * here
        new = [carry[0] + fold(here)]
        for k in range(taps):
            if k:
                total = total + conv_w[k : k + 1, :] * ahead[k : k + STEP]
            new.append(carry[k + 1] + fold(here * behind[8 - k : 8 - k + STEP]))
        d_branch[0, pl.ds(at, STEP), :] = total.astype(BF)
        tail_out[0] = total[STEP - 8 : STEP]
        return tuple(new)

    found = lax.fori_loop(0, length // STEP, conv_step, (zero,) * (taps + 1))
    for k, total in enumerate((s_decay, s_rate, s_inlet, *found)):
        sums[k] += total


def run_backward_gates(
    local_c, prod_c, carry_in, state, state_in, conv_out, branch, halo, conv_w, vectors, rate_w, inlet_w
):
    seqs, length, channels = branch.shape
    width = rate_w.shape[1]
    taps = conv_w.shape[0]
    wide = pl.BlockSpec((1, length, width), lambda j, s: (s, 0, j))
    line = pl.BlockSpec((1, 1, width), lambda j, s: (s, 0, j))
    edge = pl.BlockSpec((1, 8, width), lambda j, s: (s, 0, j))
    gate = pl.BlockSpec((1, width, width), lambda j, s: (j, 0, 0))
    edge_shape = jax.ShapeDtypeStruct((seqs, 8, channels), F32)
    gate_shape = jax.ShapeDtypeStruct(rate_w.shape, F32)
    return pl.pallas_call(
        backward_gates_kernel,
        grid=(channels // width, seqs),
        in_specs=[
            wide,
            wide,
            line,
            wide,
            line,
            wide,
            wide,
            edge,
            pl.BlockSpec((taps, width), lambda j, s: (0, j)),
            pl.BlockSpec((vectors.shape[0], width), lambda j, s: (0, j)),
            gate,
            gate,
        ],
        out_specs=[
            wide,
            edge,
            edge,
            gate,
            gate,
            pl.BlockSpec((taps + 4, 8, width), lambda j, s: (0, 0, j)),
        ],
        out_shape=[
            jax.ShapeDtypeStruct(branch.shape, BF),
            edge_shape,
            edge_shape,
            gate_shape,
            gate_shape,
            jax.ShapeDtypeStruct((taps + 4, 8, channels), F32),
        ],
        scratch_shapes=[
            pltpu.VMEM((length + 8, width), F32),
            pltpu.VMEM((length + 8, width), F32),
            pltpu.VMEM((length, width), F32),
            pltpu.VMEM((length, width), F32),
            pltpu.VMEM((length, width), BF),
            pltpu.VMEM((length, width), BF),
            pltpu.VMEM((length + 8, width), F32),
        ],
        cost_estimate=pl.CostEstimate(
            flops=100 * branch.size + 12 * branch.size * width,
            bytes_accessed=22 * branch.size,
            transcendentals=5 * branch.size,
        ),
        name="backward_gates",
    )(local_c, prod_c, carry_in, state, state_in, conv_out, branch, halo, conv_w, vectors, rate_w, inlet_w)


def rms_norm(values, gain_vec):
    inv_rms = lax.rsqrt(jnp.mean(values * values, axis=-1, keepdims=True) + EPS)
    return values * inv_rms * gain_vec


def norm_back(values, gain_vec, cot):
    inv_rms = lax.rsqrt(jnp.mean(values * values, axis=-1, keepdims=True) + EPS)
    unit = values * inv_rms
    scaled = cot * gain_vec
    grad = inv_rms * (scaled - unit * jnp.mean(scaled * unit, axis=-1, keepdims=True))
    return grad, jnp.sum(cot * unit, axis=(0, 1))


def times(values, matrix, dtype=F32):
    return jnp.einsum("slk,kn->sln", values, matrix, preferred_element_type=dtype)


def times_t(values, matrix, dtype=F32):
    return jnp.einsum("sln,kn->slk", values, matrix, preferred_element_type=dtype)


def outer_sum(values, cotangent):
    return jnp.einsum("slk,sln->kn", values, cotangent, preferred_element_type=F32).astype(BF)


def shards(
    inputs,
    teacher,
    seq_lengths,
    first_gain,
    branch_weight,
    branch_bias,
    gate_weight,
    gate_bias,
    conv_weight,
    conv_bias,
    rate_weight,
    rate_bias,
    inlet_weight,
    inlet_bias,
    decay_param,
    out_weight,
    second_gain,
    geglu_gate,
    geglu_up,
    geglu_down,
):
    seq_dev, local_len, model_width = inputs.shape
    tp = lax.axis_size("tp")
    fsdp = lax.axis_size("fsdp")
    chips = fsdp // 2
    full_len = local_len * tp
    me = lax.axis_index("fsdp")
    z = lax.axis_index("tp")
    core = me & 1
    chip = me // 2
    width = rate_weight.shape[2]
    taps = conv_weight.shape[0]

    zs = [("z", b) for b in bits_of(tp)]
    ds = [("d", b) for b in bits_of(chips)]
    order_a = zs + ds
    order_b = zs + ds[::-1]
    order_mid_a = ds[:1] + zs + ds[1:]
    order_mid_b = ds[-1:] + zs + ds[:-1]

    def same_chip(values):
        return swap(values, "fsdp", 1)

    def both_rows(values):
        return in_core_order(values, same_chip(values), core, 0)

    def unit_of(matrix, channel_axis):
        mine = pick_half(matrix, core, channel_axis)
        other = same_chip(pick_half(matrix, 1 - core, channel_axis))
        if channel_axis == 1:
            mine, other = mine.T, other.T
        return in_core_order(mine, other, core, 1)

    x4 = both_rows(inputs)
    w_branch = gather_matrix(unit_of(branch_weight, 1), order_a)
    w_gate = gather_matrix(unit_of(gate_weight, 1), order_b)

    rows_chip = 2 * rate_weight.shape[1]
    pair = jnp.concatenate([rate_weight, inlet_weight], axis=1)
    pair_mine = pick_half(pair, core, 0)[0]
    pair_other = same_chip(pick_half(pair, 1 - core, 0)[0])
    pair_unit = in_core_order(
        pair_mine.reshape(2, -1, width), pair_other.reshape(2, -1, width), core, 1
    )

    def pack_pair(values):
        return values.reshape(values.shape[0], -1)

    held = pair_unit[None]
    for b in bits_of(tp):
        held = jnp.concatenate([held, swap(held, "tp", b)], axis=0)
    held = held[:, :, None]
    for b in bits_of(chips):
        held = jnp.concatenate([held, swap(held, "fsdp", 2 * b)], axis=2)
    held = xor_blocks(held, 2, chips, chip)
    held = held.reshape(tp, 2, chips * rows_chip, width)
    w_rate, w_inlet = held[:, 0], held[:, 1]

    w_out = gather_matrix(unit_of(out_weight, 0), order_mid_b)
    w_ffgate = gather_matrix(unit_of(geglu_gate, 1), order_a)
    w_ffup = gather_matrix(unit_of(geglu_up, 1), order_b)
    w_ffdown = gather_matrix(unit_of(geglu_down, 0), order_mid_a)

    def to_relative(values):
        return xor_blocks(values, values.ndim - 1, tp, z)

    local_vectors = jnp.concatenate(
        [
            conv_weight,
            jnp.stack([branch_bias, gate_bias, conv_bias, rate_bias, inlet_bias, decay_param]),
        ],
        axis=0,
    )
    held = pick_half(local_vectors, core, 1)
    for b in bits_of(tp):
        held = jnp.concatenate([held, swap(held, "tp", b)], axis=1)
    taps_w = held[:taps]
    b_branch, b_gate, b_conv, b_rate, b_inlet, decay_vec = (held[taps + k] for k in range(6))
    soft = jax.nn.softplus(-decay_vec)
    vectors = jnp.stack([b_conv, b_rate, b_inlet, soft])

    lengths4 = both_rows(seq_lengths)
    count = jnp.broadcast_to(jnp.sum(lengths4.astype(F32)), (8, 128))
    for b in bits_of(chips):
        count = count + swap(count, "fsdp", 2 * b)
    valid_total = count[0, 0]

    def to_chip(values):
        return xor_blocks(values, values.ndim - 1, chips, chip)

    gain1, gain2 = to_chip(first_gain), to_chip(second_gain)
    x4 = to_chip(x4)
    residual = x4.astype(F32)
    first_rows = rms_norm(residual, gain1).astype(BF)
    branch_pre = times_t(first_rows, w_branch) + b_branch
    gate_pre = times_t(first_rows, w_gate) + b_gate

    def along_z(values, shift):
        pairs = [(i, i + shift) for i in range(tp) if 0 <= i + shift < tp]
        return to_relative(lax.ppermute(to_relative(values), "tp", pairs))

    halo = jnp.pad(along_z(branch_pre[:, local_len - taps + 1 :], 1), ((0, 0), (8 - taps + 1, 0), (0, 0)))
    conv_out, decay_rate, local_state, prod_decay = run_forward(
        branch_pre, halo, taps_w, vectors, w_rate, w_inlet
    )
    ends = jnp.stack([prod_decay[:, -1], local_state[:, -1]])
    state_in = jnp.zeros_like(ends[0])
    for shift in reversed(range(1, tp)):
        got = along_z(ends, shift)
        state_in = got[1] + got[0] * state_in
    state_in = state_in[:, None]
    state = local_state + prod_decay * state_in
    mixed = (state * jax.nn.gelu(gate_pre)).astype(BF)

    def core_sum(term):
        return term.astype(F32) + same_chip(term).astype(F32)

    middle = residual + core_sum(times(mixed, w_out, BF))
    second_rows = rms_norm(middle, gain2).astype(BF)
    ff_gate = times_t(second_rows, w_ffgate)
    ff_up = times_t(second_rows, w_ffup)
    ff_hidden = (jax.nn.gelu(ff_gate) * ff_up).astype(BF)
    final = middle + core_sum(times(ff_hidden, w_ffdown, BF))

    positions = z * local_len + jnp.arange(local_len, dtype=jnp.int32)
    valid_mask = (positions[None, :] < lengths4[:, None]).astype(F32)[..., None]
    teacher4 = to_chip(both_rows(teacher)).astype(F32)
    mismatch = final - teacher4
    loss_part = jnp.sum(valid_mask * mismatch * mismatch)
    scaling = seq_dev * fsdp * full_len / valid_total
    out_cot = valid_mask * mismatch * scaling
    ff_cot = out_cot.astype(BF)

    g_ffdown = scatter_matrix(outer_sum(ff_hidden, ff_cot), order_mid_a, chips)
    d_hidden = times_t(ff_cot, w_ffdown)
    act, slope = gelu_parts(ff_gate)
    d_up = (d_hidden * act).astype(BF)
    d_ffgate = (d_hidden * ff_up * slope).astype(BF)
    g_ffgate = scatter_matrix(outer_sum(d_ffgate, second_rows), order_a, chips)
    g_ffup = scatter_matrix(outer_sum(d_up, second_rows), order_b, chips)
    d_second = core_sum((times(d_ffgate, w_ffgate) + times(d_up, w_ffup)).astype(BF))
    d_mid_norm, g_second = norm_back(middle, gain2, d_second)
    d_middle = out_cot + d_mid_norm
    mid_cot = d_middle.astype(BF)
    d_mixed = times_t(mid_cot, w_out)
    g_out = scatter_matrix(outer_sum(mixed, mid_cot), order_mid_b, chips)
    d_gate, local_c, prod_c = run_backward_scan(d_mixed, gate_pre, state, decay_rate, width)
    starts = jnp.stack([prod_c[:, 0], local_c[:, 0]]) * decay_rate[:, 0]
    carry_in = jnp.zeros_like(starts[0])
    for shift in reversed(range(1, tp)):
        got = along_z(starts, -shift)
        carry_in = got[1] + got[0] * carry_in
    g_gate = scatter_matrix(outer_sum(d_gate, first_rows), order_b, chips)
    d_branch, head, tail, g_rate, g_inlet, sums = run_backward_gates(
        local_c,
        prod_c,
        carry_in[:, None],
        state,
        state_in,
        conv_out,
        branch_pre,
        halo,
        taps_w,
        vectors,
        w_rate,
        w_inlet,
    )
    ahead = along_z(head[:, : taps - 1], -1)
    edge = tail[:, 8 - taps + 1 :]
    for k in range(1, taps):
        first = taps - 1 - k
        edge = edge.at[:, first:].add(taps_w[k] * ahead[:, :k])
    d_branch = lax.dynamic_update_slice(d_branch, edge.astype(BF), (0, local_len - taps + 1, 0))
    g_branch = scatter_matrix(outer_sum(d_branch, first_rows), order_a, chips)
    d_first_part = (times(d_branch, w_branch) + times(d_gate, w_gate)).astype(BF)

    def own(values):
        return pick_half(values, core, 0)

    d_first = own(d_first_part).astype(F32) + same_chip(pick_half(d_first_part, 1 - core, 0)).astype(F32)
    d_in_norm, g_first = norm_back(inputs_rel := own(residual), gain1, d_first)
    input_grad = to_chip(own(d_middle) + d_in_norm)
    block_out = to_chip(own(final).astype(BF))

    pair_g = jnp.stack([g_rate, g_inlet], axis=1).astype(BF)
    pair_g = pair_g.reshape(tp, 2, chips, rows_chip, width)
    pair_g = xor_blocks(pair_g, 2, chips, chip)
    for b in reversed(bits_of(chips)):
        keep, send = jnp.split(pair_g, 2, axis=2)
        pair_g = (keep.astype(F32) + swap(send, "fsdp", 2 * b).astype(F32)).astype(BF)
    for b in reversed(bits_of(tp)):
        keep, send = jnp.split(pair_g, 2, axis=0)
        pair_g = keep.astype(F32) + swap(send, "tp", b).astype(F32)
        if b > 1:
            pair_g = pair_g.astype(BF)
    pair_g = pair_g.reshape(2, rows_chip, width)
    pair_mine = pick_half(pair_g, core, 1)
    pair_other = same_chip(pick_half(pair_g, 1 - core, 1))
    pair_g = in_core_order(pair_mine[None], pair_other[None], core, 0)

    def to_own(grad, channel_axis):
        mine = pick_half(grad, core, 1)
        other = same_chip(pick_half(grad, 1 - core, 1))
        whole = in_core_order(mine, other, core, 0)
        return whole.T if channel_axis == 1 else whole

    sums = jnp.sum(sums, axis=1)
    small = jnp.concatenate(
        [
            jnp.stack(
                [
                    jnp.sum(d_branch.astype(F32), axis=(0, 1)),
                    jnp.sum(d_gate.astype(F32), axis=(0, 1)),
                    sums[0] * (DECAY_SCALE * jax.nn.sigmoid(-decay_vec)),
                ]
            ),
            sums[1:],
        ],
        axis=0,
    )
    for b in bits_of(chips):
        small = small + swap(small, "fsdp", 2 * b)
    for b in reversed(bits_of(tp)):
        keep, send = jnp.split(small, 2, axis=1)
        small = keep + swap(send, "tp", b)
    small = in_core_order(small, same_chip(small), core, 1)
    stats = jnp.stack(
        [
            jnp.broadcast_to(0.5 * loss_part, (model_width,)),
            to_chip(g_first),
            to_chip(0.5 * g_second),
        ]
    )
    for b in bits_of(fsdp):
        stats = stats + swap(stats, "fsdp", b)
    for b in bits_of(tp):
        stats = stats + swap(stats, "tp", b)
    loss_value = stats[0, 0] / (model_width * valid_total)
    return (
        block_out,
        loss_value,
        input_grad,
        stats[1],
        to_own(g_branch, 1),
        small[0],
        to_own(g_gate, 1),
        small[1],
        small[6:],
        small[5],
        pair_g[:, 0],
        small[3],
        pair_g[:, 1],
        small[4],
        small[2],
        to_own(g_out, 0),
        stats[2],
        to_own(g_ffgate, 1),
        to_own(g_ffup, 1),
        to_own(g_ffdown, 0),
    )


def solution(mesh):
    rows = P("fsdp", "tp", None)
    by_column, by_row = P("fsdp", "tp"), P("tp", "fsdp")
    blocks = P("tp", "fsdp", None)
    channel = P("tp")
    return jax.shard_map(
        shards,
        mesh=mesh,
        in_specs=(
            rows,
            rows,
            P("fsdp"),
            P(),
            by_column,
            channel,
            by_column,
            channel,
            P(None, "tp"),
            channel,
            blocks,
            channel,
            blocks,
            channel,
            channel,
            by_row,
            P(),
            by_column,
            by_column,
            by_row,
        ),
        out_specs=(
            rows,
            P(),
            rows,
            P(),
            by_column,
            channel,
            by_column,
            channel,
            P(None, "tp"),
            channel,
            blocks,
            channel,
            blocks,
            channel,
            channel,
            by_row,
            P(),
            by_column,
            by_column,
            by_row,
        ),
        check_vma=False,
    )
```

time: 2570 us -> 1200 us (0.47)
  waiting for transfers between devices: 1560 us -> 564 us
  local copies, waits for them, and re-layouts: 472 us -> 76.1 us
  blocking collectives: 103 us -> 0 us
  starting transfers between devices: 1.32 us -> 101 us
  Pallas kernels: 0 us -> 83.2 us
    reduce_scatter x12 -> x0, waiting for transfers between devices: 1110 us -> none  [the longest x4 724 us: reduce_rows(): lax.psum_scatter(make_term(0, full_len), 'tp', scatter_dimension=1, tiled...]
    ppermute x0 -> x99, waiting for transfers between devices: none -> 564 us  [the longest x91 553 us: swap(): return lax.ppermute(values, axis_name, [(i, i ^ bit) for i in range(size)])]
    all_gather x10 -> x0, waiting for transfers between devices: 452 us -> none  [the longest x4 378 us: gather_rows(): return lax.all_gather(values, 'tp', axis=1, tiled=True)]
    slice x128 -> x24, local copies, waits for them, and re-layouts: 328 us -> 28.5 us  [the longest x12 15.7 us: lane_blocks(): runs.append(values[:, wanted[start] * width:(wanted[stop - 1] + 1) * width])]
    ppermute x0 -> x99, starting transfers between devices: none -> 101 us  [the longest x91 84.7 us: swap(): return lax.ppermute(values, axis_name, [(i, i ^ bit) for i in range(size)])]
    pallas_call x0 -> x3, Pallas kernels: none -> 83.2 us  [the longest x1 37.7 us: run_backward_gates(): pl.pallas_call(backward_gates_kernel, grid=(channels // width, seqs), in_...]
    psum x3 -> x0, blocking collectives: 82 us -> none  [the longest x1 42.3 us: shards(): stats = lax.psum((loss_part, g_first, g_second), ('fsdp', 'tp'))]
    pad x36 -> x0, local copies, waits for them, and re-layouts: 51.1 us -> none  [linear_scan(): return lax.associative_scan(combine, (decay_rate, source), axis=1)[1]]
  transfers between devices with their start and end apart: 22 -> 99, of which waited for: 20 -> 48; matrix products, arithmetic and copies ran while one was open for 18% -> 32% of each run, Pallas kernels for 0% -> 7%
where the time goes in v1:
time: 1200 us
  waiting for transfers between devices  564 us (47%)
  matrix products  216 us (18%)
  other arithmetic  148 us (12%)
  starting transfers between devices  101 us (8%)
  Pallas kernels  83.2 us (7%)
  local copies, waits for them, and re-layouts  76.1 us (6%)
    ppermute x91, waiting for transfers between devices, swap(): return lax.ppermute(values, axis_name, [(i, i ^ bit) for i in range(size)])  553 us
    dot_general x6, matrix products, times_t(): jnp.einsum('sln,kn->slk', values, matrix, preferred_element_type=dtype)  85.1 us
    ppermute x91, starting transfers between devices, swap(): return lax.ppermute(values, axis_name, [(i, i ^ bit) for i in range(size)])  84.7 us
    dot_general x6, matrix products, times(): jnp.einsum('slk,kn->sln', values, matrix, preferred_element_type=dtype)  75.3 us
    dot_general x6, matrix products, outer_sum(): jnp.einsum('slk,sln->kn', values, cotangent, preferred_element_type=F32)  55.8 us
    pallas_call x1, Pallas kernels, run_backward_gates(): pl.pallas_call(backward_gates_kernel, grid=(channels // width, seqs), in_...  37.7 us
    pallas_call x1, Pallas kernels, run_forward(): pl.pallas_call(forward_kernel, grid=(channels // width, seqs), in_specs=[...  27.5 us
  transfers between devices with their start and end apart: 99, of which 48 were waited for; matrix products, arithmetic and copies ran while one was open for 32% of the time, Pallas kernels for 7%

profile of v1, /device:TPU:0, one launch (start us, length us, event | category | flops | bytes accessed | tf_op | source)
XLA Modules:
  0.0 1195.1 jit_solution(3034599776785865902)
XLA Ops:
  51.9 14.0 %collective-permute-done.29 = bf16[576,384]{1,0:T(8,128)(2,1)S(1)} collective-permute-done((bf16[576,384]{1,0:T(8,128)(2,1)S(1)}, bf16[576,384]{1,0:T(8,128)(2,1)S(1)}, u32[]{:S(2)}, u32[]{:S(2)}) %collective-permute-start.29) | collective-permute-done | bytes 442400 | tf_op jit(solution)/shard_map/ppermute | solution.py:21
  113.9 55.1 %collective-permute-done.25 = bf16[512,768]{1,0:T(8,128)(2,1)S(1)} collective-permute-done((bf16[512,768]{1,0:T(8,128)(2,1)S(1)}, bf16[512,768]{1,0:T(8,128)(2,1)S(1)}, u32[]{:S(2)}, u32[]{:S(2)}) %collective-permute-start.25) | collective-permute-done | bytes 786464 | tf_op jit(solution)/shard_map/ppermute | solution.py:21
  173.1 14.9 %collective-permute-done.30 = bf16[1152,384]{1,0:T(8,128)(2,1)S(1)} collective-permute-done((bf16[1152,384]{1,0:T(8,128)(2,1)S(1)}, bf16[1152,384]{1,0:T(8,128)(2,1)S(1)}, u32[]{:S(2)}, u32[]{:S(2)}) %collective-permute-start.30) | collective-permute-done | bytes 884768 | tf_op jit(solution)/shard_map/ppermute | solution.py:21
  198.0 27.9 %collective-permute-done.5 = bf16[1024,768]{1,0:T(8,128)(2,1)S(1)} collective-permute-done((bf16[1024,768]{1,0:T(8,128)(2,1)S(1)}, bf16[1024,768]{1,0:T(8,128)(2,1)S(1)}, u32[]{:S(2)}, u32[]{:S(2)}) %collective-permute-start.5) | collective-permute-done | bytes 1572896 | tf_op jit(solution)/shard_map/ppermute | solution.py:21
  232.5 26.7 %collective-permute-done.21 = bf16[1024,768]{1,0:T(8,128)(2,1)S(1)} collective-permute-done((bf16[1024,768]{1,0:T(8,128)(2,1)S(1)}, bf16[1024,768]{1,0:T(8,128)(2,1)S(1)}, u32[]{:S(2)}, u32[]{:S(2)}) %collective-permute-start.21) | collective-permute-done | bytes 1572896 | tf_op jit(solution)/shard_map/ppermute | solution.py:21
  263.1 27.5 %forward_scan.1 = (bf16[4,256,1024]{2,1,0:T(8,128)(2,1)}, f32[4,256,1024]{2,1,0:T(8,128)}, f32[4,256,1024]{2,1,0:T(8,128)}, f32[4,256,1024]{2,1,0:T(8,128)}) custom-call(f32[4,256,1024]{2,1,0:T(8,128)} %copy-done.42, f32[4,8,1024]{2,1,0:T(8,128)} %select_maximum_fusion.halo, f32[4,1024]{1,0:T(4,128)} %slice.432.conv_w, ...), custom_call_target="tpu_custom_call" | custom-call | flops 1136656384 | bytes 20971520 | tf_op jit(solution)/shard_map/forward_scan/pallas_call | solution.py:186
  344.6 23.3 %collective-permute-done.36 = bf16[2304,384]{1,0:T(8,128)(2,1)S(1)} collective-permute-done((bf16[2304,384]{1,0:T(8,128)(2,1)S(1)}, bf16[2304,384]{1,0:T(8,128)(2,1)S(1)}, u32[]{:S(2)}, u32[]{:S(2)}) %collective-permute-start.36) | collective-permute-done | bytes 1769504 | tf_op jit(solution)/shard_map/ppermute | solution.py:21
  376.9 31.5 %collective-permute-done.41 = bf16[1152,768]{1,0:T(8,128)(2,1)S(1)} collective-permute-done((bf16[1152,768]{1,0:T(8,128)(2,1)S(1)}, bf16[1152,768]{1,0:T(8,128)(2,1)S(1)}, u32[]{:S(2)}, u32[]{:S(2)}) %collective-permute-start.41) | collective-permute-done | bytes 1769504 | tf_op jit(solution)/shard_map/ppermute | solution.py:21
  422.5 21.3 %collective-permute-done.32 = bf16[2304,768]{1,0:T(8,128)(2,1)} collective-permute-done((bf16[2304,768]{1,0:T(8,128)(2,1)S(1)}, bf16[2304,768]{1,0:T(8,128)(2,1)}, u32[]{:S(2)}, u32[]{:S(2)}) %collective-permute-start.32) | collective-permute-done | bytes 3538976 | tf_op jit(solution)/shard_map/ppermute | solution.py:21
  443.8 19.4 %fusion.37 = f32[4,256,2304]{2,1,0:T(8,128)} fusion(bf16[4,256,1536]{2,1,0:T(8,128)(2,1)} %multiply_convert_fusion.1, bf16[2304,768]{1,0:T(8,128)(2,1)} %collective-permute-done.32, bf16[2304,384]{1,0:T(8,128)(2,1)} %collective-permute-done.31, bf16[1152,384]{1,0:T(8,128)(2,1)S(1)} %copy-done.53, bf16[576,384]{1,0:T(8,128)(2,1)S(1)} %copy-done.44, ...), kind=kOutput, calls=%fused_computation.139 | convolution fusion | flops 7290224640 | bytes 19660800 | tf_op jit(solution)/shard_map/sln,kn->slk/dot_general | solution.py:461
  466.4 18.6 %fusion.8 = (bf16[4,256,2304]{2,1,0:T(8,128)(2,1)}, f32[4,256,2304]{2,1,0:T(8,128)}) fusion(f32[4,256,2304]{2,1,0:T(8,128)} %fusion.37, bf16[4,256,1536]{2,1,0:T(8,128)(2,1)S(1)} %copy-done.67, bf16[2304,384]{1,0:T(8,128)(2,1)} %get-tuple-element.177, bf16[2304,384]{1,0:T(8,128)(2,1)} %copy-done.77, bf16[2304,384]{1,0:T(8,128)(2,1)} %get-tuple-element.176, ...), kind=kOutput, calls=%fused_computation.14 | convolution fusion | flops 7320895488 | bytes 33816576 | tf_op jit(solution)/shard_map/sln,kn->slk/dot_general | solution.py:461
  484.9 34.0 %collective-permute-done.42 = bf16[2304,768]{1,0:T(8,128)(2,1)} collective-permute-done((bf16[2304,768]{1,0:T(8,128)(2,1)S(1)}, bf16[2304,768]{1,0:T(8,128)(2,1)}, u32[]{:S(2)}, u32[]{:S(2)}) %collective-permute-start.42) | collective-permute-done | bytes 3538976 | tf_op jit(solution)/shard_map/ppermute | solution.py:21
  519.0 20.9 %fusion.39 = bf16[4,256,1536]{2,1,0:T(8,128)(2,1)} fusion(bf16[4,256,2304]{2,1,0:T(8,128)(2,1)} %get-tuple-element.339, bf16[2304,768]{1,0:T(8,128)(2,1)} %collective-permute-done.42, bf16[1152,768]{1,0:T(8,128)(2,1)S(1)} %copy-done.80, bf16[576,768]{1,0:T(8,128)(2,1)} %collective-permute-done.40, bf16[576,384]{1,0:T(8,128)(2,1)S(1)} %copy-done.50, ...), kind=kOutput, calls=%fused_computation.141 | convolution fusion | flops 7290224640 | bytes 14942208 | tf_op jit(solution)/shard_map/slk,kn->sln/dot_general | solution.py:457
  570.2 14.2 %bitcast_convert_fusion = bf16[2304,1536]{1,0:T(8,128)(2,1)S(1)} fusion(bf16[4,256,2304]{2,1,0:T(8,128)(2,1)} %get-tuple-element.339, f32[]{:T(128)} %bitcast.32, f32[4,256]{1,0:T(4,128)S(1)} %compare_convert_fusion, f32[4,256,1536]{2,1,0:T(8,128)S(1)} %get-tuple-element.142, bf16[4,256,384]{2,1,0:T(8,128)(2,1)S(1)} %get-tuple-element.197, ...), kind=kOutput, calls=%fused_computation | convolution fusion | flops 7270170624 | bytes 21237764 | tf_op jit(solution)/shard_map/slk,sln->kn/dot_general | solution.py:465
  589.0 26.4 %fusion.17 = (bf16[4,256,2304]{2,1,0:T(8,128)(2,1)}, bf16[4,256,2304]{2,1,0:T(8,128)(2,1)}) fusion(f32[4,256,2304]{2,1,0:T(8,128)} %fusion.37, f32[4,256,2304]{2,1,0:T(8,128)} %get-tuple-element.340, bf16[2304,768]{1,0:T(8,128)(2,1)} %collective-permute-done.42, bf16[1152,768]{1,0:T(8,128)(2,1)} %copy-done.79, ...), kind=kOutput, calls=%fused_computation.23 | convolution fusion | flops 7361003520 | bytes 44830724 | tf_op jit(solution)/shard_map/sln,kn->slk/dot_general | solution.py:461
  633.1 15.5 %fusion.48 = f32[4,256,1536]{2,1,0:T(8,128)} fusion(bf16[4,256,2304]{2,1,0:T(8,128)(2,1)} %get-tuple-element.167, bf16[2304,384]{1,0:T(8,128)(2,1)S(1)} %copy-done.82, bf16[2304,384]{1,0:T(8,128)(2,1)S(1)} %copy-done.78, bf16[2304,384]{1,0:T(8,128)(2,1)S(1)} %copy-done.81, bf16[1152,384]{1,0:T(8,128)(2,1)} %collective-permute-done.35, ...), kind=kOutput, calls=%fused_computation.219 | convolution fusion | flops 7297302528 | bytes 18087936 | tf_op jit(solution)/shard_map/slk,kn->sln/dot_general | solution.py:457
  648.6 15.7 %add_convert_fusion.4 = bf16[4,256,1536]{2,1,0:T(8,128)(2,1)} fusion(f32[4,256,1536]{2,1,0:T(8,128)} %fusion.48, bf16[4,256,2304]{2,1,0:T(8,128)(2,1)S(1)} %bitcast.201, bf16[2304,768]{1,0:T(8,128)(2,1)} %collective-permute-done.32, bf16[2304,384]{1,0:T(8,128)(2,1)} %collective-permute-done.31, bf16[1152,384]{1,0:T(8,128)(2,1)S(1)} %copy-done.54, ...), kind=kOutput, calls=%fused_computation.43 | convolution fusion | flops 7293370368 | bytes 21233664 | tf_op jit(solution)/shard_map/slk,kn->sln/dot_general | solution.py:457
  708.5 18.0 %backward_scan.1 = (bf16[4,256,1024]{2,1,0:T(8,128)(2,1)}, f32[4,256,1024]{2,1,0:T(8,128)}, f32[4,256,1024]{2,1,0:T(8,128)}) custom-call(f32[4,256,1024]{2,1,0:T(8,128)} %fusion.34.d_mixed, f32[4,256,1024]{2,1,0:T(8,128)} %get-tuple-element.338.gate_pre, f32[4,256,1024]{2,1,0:T(8,128)} %get-tuple-element.156.state, f32[4,256,1024]{2,1,0:T(8,128)} %get-tuple-element.79.decay), custom_call_target="tpu_custom_call" | custom-call | flops 62914560 | bytes 25165824 | tf_op jit(solution)/shard_map/backward_scan/pallas_call | solution.py:258
  766.4 37.7 %backward_gates.1 = (bf16[4,256,1024]{2,1,0:T(8,128)(2,1)}, f32[4,8,1024]{2,1,0:T(8,128)}, f32[4,8,1024]{2,1,0:T(8,128)}, f32[4,256,256]{2,1,0:T(8,128)}, f32[4,256,256]{2,1,0:T(8,128)}, /*index=5*/f32[8,8,1024]{2,1,0:T(8,128)}) custom-call(f32[4,256,1024]{2,1,0:T(8,128)} %get-tuple-element.80.local_c, f32[4,256,1024]{2,1,0:T(8,128)} %get-tuple-element.81.prod_c, ...), custom_call_target="tpu_custom_call" | custom-call | flops 3326083072 | bytes 23068672 | tf_op jit(solution)/shard_map/backward_gates/pallas_call | solution.py:392
  854.1 35.6 %collective-permute-done.75 = bf16[4,2,1,64,256]{4,3,1,2,0:T(8,128)(2,1)S(1)} collective-permute-done((bf16[4,2,1,64,256]{4,3,1,2,0:T(8,128)(2,1)S(1)}, bf16[4,2,1,64,256]{4,3,1,2,0:T(8,128)(2,1)S(1)}, u32[]{:S(2)}, u32[]{:S(2)}) %collective-permute-start.75) | collective-permute-done | bytes 262176 | tf_op jit(solution)/shard_map/ppermute | solution.py:21
  939.8 21.5 %collective-permute-done.55 = f32[3,1536]{1,0:T(4,128)S(1)} collective-permute-done((f32[3,1536]{1,0:T(4,128)S(1)}, f32[3,1536]{1,0:T(4,128)S(1)}, u32[]{:S(2)}, u32[]{:S(2)}) %collective-permute-start.55) | collective-permute-done | bytes 18464 | tf_op jit(solution)/shard_map/ppermute | solution.py:21
  980.6 44.9 %collective-permute-done.58 = f32[3,1536]{1,0:T(4,128)S(1)} collective-permute-done((f32[3,1536]{1,0:T(4,128)S(1)}, f32[3,1536]{1,0:T(4,128)S(1)}, u32[]{:S(2)}, u32[]{:S(2)}) %collective-permute-start.58) | collective-permute-done | bytes 18464 | tf_op jit(solution)/shard_map/ppermute | solution.py:21
  1049.1 50.1 %collective-permute-done.81 = bf16[256,768]{1,0:T(8,128)(2,1)S(1)} collective-permute-done((bf16[256,768]{1,0:T(8,128)(2,1)S(1)}, bf16[256,768]{1,0:T(8,128)(2,1)S(1)}, u32[]{:S(2)}, u32[]{:S(2)}) %collective-permute-start.81) | collective-permute-done | bytes 393248 | tf_op jit(solution)/shard_map/ppermute | solution.py:21
  1103.2 38.0 %collective-permute-done.71 = bf16[512,384]{1,0:T(8,128)(2,1)S(1)} collective-permute-done((bf16[512,384]{1,0:T(8,128)(2,1)S(1)}, bf16[512,384]{1,0:T(8,128)(2,1)S(1)}, u32[]{:S(2)}, u32[]{:S(2)}) %collective-permute-start.71) | collective-permute-done | bytes 393248 | tf_op jit(solution)/shard_map/ppermute | solution.py:21
  (802 shorter events, 534.6 us)
Async XLA Ops:
  5.3 184.8 %collective-permute-start = (bf16[2,256,1536]{2,1,0:T(8,128)(2,1)}, bf16[2,256,1536]{2,1,0:T(8,128)(2,1)}, u32[]{:S(2)}, u32[]{:S(2)}) collective-permute-start(bf16[2,256,1536]{2,1,0:T(8,128)(2,1)} %param.28), channel_id=1, source_target_pairs={{0,4},{4,0},{8,12},{12,8},{16,20},{20,16},{24,28},{28,24},{1,5},{5... | collective-permute-start | bytes 4718600 | tf_op jit(solution)/shard_map/ppermute | solution.py:21
  78.6 111.9 %collective-permute-start.45 = (bf16[2,256,1536]{2,1,0:T(8,128)(2,1)S(1)}, bf16[2,256,1536]{2,1,0:T(8,128)(2,1)S(1)}, u32[]{:S(2)}, u32[]{:S(2)}) collective-permute-start(bf16[2,256,1536]{2,1,0:T(8,128)(2,1)S(1)} %copy-done.88), channel_id=1, source_target_pairs={{0,4},{4,0},{8,12},{12,8},{16,20},{20,16},{24,28},{28,24},{1,5},{5... | collective-permute-start | bytes 4718600 | tf_op jit(solution)/shard_map/ppermute | solution.py:21
  95.2 73.8 %collective-permute-start.25 = (bf16[512,768]{1,0:T(8,128)(2,1)S(1)}, bf16[512,768]{1,0:T(8,128)(2,1)S(1)}, u32[]{:S(2)}, u32[]{:S(2)}) collective-permute-start(bf16[512,768]{1,0:T(8,128)(2,1)S(1)} %pad_maximum_fusion.24), channel_id=1, source_target_pairs={{0,2},{1,3},{2,0},{3,1},{4,6},{5,7},{6,4},{7,5},{8,10},{9,11},{10,... | collective-permute-start | bytes 2359304 | tf_op jit(solution)/shard_map/ppermute | solution.py:21
  109.4 78.6 %collective-permute-start.30 = (bf16[1152,384]{1,0:T(8,128)(2,1)S(1)}, bf16[1152,384]{1,0:T(8,128)(2,1)S(1)}, u32[]{:S(2)}, u32[]{:S(2)}) collective-permute-start(bf16[1152,384]{1,0:T(8,128)(2,1)S(1)} %pad_maximum_fusion.17), channel_id=1, source_target_pairs={{0,2},{1,3},{2,0},{3,1},{4,6},{5,7},{6,4},{7,5},{8,10},{9,11},{10,... | collective-permute-start | bytes 2654216 | tf_op jit(solution)/shard_map/ppermute | solution.py:21
  111.5 213.1 %collective-permute-start.35 = (bf16[1152,384]{1,0:T(8,128)(2,1)}, bf16[1152,384]{1,0:T(8,128)(2,1)}, u32[]{:S(2)}, u32[]{:S(2)}) collective-permute-start(bf16[1152,384]{1,0:T(8,128)(2,1)} %pad_maximum_fusion.18), channel_id=1, source_target_pairs={{0,2},{1,3},{2,0},{3,1},{4,6},{5,7},{6,4},{7,5},{8,10},{9,11},{10,... | collective-permute-start | bytes 2654216 | tf_op jit(solution)/shard_map/ppermute | solution.py:21
  169.0 157.9 %collective-permute-start.40 = (bf16[576,768]{1,0:T(8,128)(2,1)}, bf16[576,768]{1,0:T(8,128)(2,1)}, u32[]{:S(2)}, u32[]{:S(2)}) collective-permute-start(bf16[576,768]{1,0:T(8,128)(2,1)} %pad_maximum_fusion.19), channel_id=1, source_target_pairs={{0,1},{1,0},{2,3},{3,2},{4,5},{5,4},{6,7},{7,6},{8,9},{9,8},{10,11... | collective-permute-start | bytes 2654216 | tf_op jit(solution)/shard_map/ppermute | solution.py:21
  188.0 110.5 %collective-permute-start.26 = (bf16[1024,768]{1,0:T(8,128)(2,1)}, bf16[1024,768]{1,0:T(8,128)(2,1)}, u32[]{:S(2)}, u32[]{:S(2)}) collective-permute-start(bf16[1024,768]{1,0:T(8,128)(2,1)} %pad_maximum_fusion.11), channel_id=1, source_target_pairs={{0,8},{4,12},{8,0},{12,4},{16,24},{20,28},{24,16},{28,20},{1,9},{5... | collective-permute-start | bytes 4718600 | tf_op jit(solution)/shard_map/ppermute | solution.py:21
  225.9 105.7 %collective-permute-start.31 = (bf16[2304,384]{1,0:T(8,128)(2,1)}, bf16[2304,384]{1,0:T(8,128)(2,1)}, u32[]{:S(2)}, u32[]{:S(2)}) collective-permute-start(bf16[2304,384]{1,0:T(8,128)(2,1)} %pad_maximum_fusion.6), channel_id=1, source_target_pairs={{0,8},{4,12},{8,0},{12,4},{16,24},{20,28},{24,16},{28,20},{1,9},{5... | collective-permute-start | bytes 5308424 | tf_op jit(solution)/shard_map/ppermute | solution.py:21
  324.6 92.1 %collective-permute-start.27 = (bf16[4,256,1536]{2,1,0:T(8,128)(2,1)S(1)}, bf16[4,256,1536]{2,1,0:T(8,128)(2,1)S(1)}, u32[]{:S(2)}, u32[]{:S(2)}) collective-permute-start(bf16[4,256,1536]{2,1,0:T(8,128)(2,1)S(1)} %fusion.36), channel_id=1, source_target_pairs={{0,4},{4,0},{8,12},{12,8},{16,20},{20,16},{24,28},{28,24},{1,5},{5... | collective-permute-start | bytes 9437192 | tf_op jit(solution)/shard_map/ppermute | solution.py:21
  328.3 80.0 %collective-permute-start.41 = (bf16[1152,768]{1,0:T(8,128)(2,1)S(1)}, bf16[1152,768]{1,0:T(8,128)(2,1)S(1)}, u32[]{:S(2)}, u32[]{:S(2)}) collective-permute-start(bf16[1152,768]{1,0:T(8,128)(2,1)S(1)} %pad_maximum_fusion.8), channel_id=1, source_target_pairs={{0,2},{1,3},{2,0},{3,1},{4,6},{5,7},{6,4},{7,5},{8,10},{9,11},{10,... | collective-permute-start | bytes 5308424 | tf_op jit(solution)/shard_map/ppermute | solution.py:21
  343.0 100.8 %collective-permute-start.32 = (bf16[2304,768]{1,0:T(8,128)(2,1)S(1)}, bf16[2304,768]{1,0:T(8,128)(2,1)}, u32[]{:S(2)}, u32[]{:S(2)}) collective-permute-start(bf16[2304,768]{1,0:T(8,128)(2,1)S(1)} %pad_maximum_fusion), channel_id=1, source_target_pairs={{0,16},{4,20},{8,24},{12,28},{16,0},{20,4},{24,8},{28,12},{1,17},{... | collective-permute-start | bytes 10616840 | tf_op jit(solution)/shard_map/ppermute | solution.py:21
  375.4 87.8 %collective-permute-start.37 = (bf16[2304,768]{1,0:T(8,128)(2,1)}, bf16[2304,768]{1,0:T(8,128)(2,1)S(1)}, u32[]{:S(2)}, u32[]{:S(2)}) collective-permute-start(bf16[2304,768]{1,0:T(8,128)(2,1)} %pad_maximum_fusion.1), channel_id=1, source_target_pairs={{0,8},{4,12},{8,0},{12,4},{16,24},{20,28},{24,16},{28,20},{1,9},{5... | collective-permute-start | bytes 10616840 | tf_op jit(solution)/shard_map/ppermute | solution.py:21
  415.2 103.8 %collective-permute-start.42 = (bf16[2304,768]{1,0:T(8,128)(2,1)S(1)}, bf16[2304,768]{1,0:T(8,128)(2,1)}, u32[]{:S(2)}, u32[]{:S(2)}) collective-permute-start(bf16[2304,768]{1,0:T(8,128)(2,1)S(1)} %pad_maximum_fusion.2), channel_id=1, source_target_pairs={{0,16},{4,20},{8,24},{12,28},{16,0},{20,4},{24,8},{28,12},{1,17},{... | collective-permute-start | bytes 10616840 | tf_op jit(solution)/shard_map/ppermute | solution.py:21
  588.4 302.0 %collective-permute-start.94 = (bf16[2304,768]{1,0:T(8,128)(2,1)}, bf16[2304,768]{1,0:T(8,128)(2,1)}, u32[]{:S(2)}, u32[]{:S(2)}) collective-permute-start(bf16[2304,768]{1,0:T(8,128)(2,1)} %slice.501), channel_id=1, source_target_pairs={{0,16},{4,20},{8,24},{12,28},{16,0},{20,4},{24,8},{28,12},{1,17},{... | collective-permute-start | bytes 10616840 | tf_op jit(solution)/shard_map/ppermute | solution.py:21
  631.1 271.7 %collective-permute-start.89 = (bf16[2304,768]{1,0:T(8,128)(2,1)}, bf16[2304,768]{1,0:T(8,128)(2,1)}, u32[]{:S(2)}, u32[]{:S(2)}) collective-permute-start(bf16[2304,768]{1,0:T(8,128)(2,1)} %pad_maximum_fusion.3), channel_id=1, source_target_pairs={{0,8},{4,12},{8,0},{12,4},{16,24},{20,28},{24,16},{28,20},{1,9},{5... | collective-permute-start | bytes 10616840 | tf_op jit(solution)/shard_map/ppermute | solution.py:21
  676.5 221.9 %collective-permute-start.84 = (bf16[2304,768]{1,0:T(8,128)(2,1)}, bf16[2304,768]{1,0:T(8,128)(2,1)}, u32[]{:S(2)}, u32[]{:S(2)}) collective-permute-start(bf16[2304,768]{1,0:T(8,128)(2,1)} %slice.491), channel_id=1, source_target_pairs={{0,16},{4,20},{8,24},{12,28},{16,0},{20,4},{24,8},{28,12},{1,17},{... | collective-permute-start | bytes 10616840 | tf_op jit(solution)/shard_map/ppermute | solution.py:21
  911.1 117.7 %collective-permute-start.95 = (bf16[1152,768]{1,0:T(8,128)(2,1)}, bf16[1152,768]{1,0:T(8,128)(2,1)}, u32[]{:S(2)}, u32[]{:S(2)}) collective-permute-start(bf16[1152,768]{1,0:T(8,128)(2,1)} %split.817), channel_id=1, source_target_pairs={{0,2},{1,3},{2,0},{3,1},{4,6},{5,7},{6,4},{7,5},{8,10},{9,11},{10,... | collective-permute-start | bytes 5308424 | tf_op jit(solution)/shard_map/ppermute | solution.py:21
  914.5 117.7 %collective-permute-start.90 = (bf16[2304,384]{1,0:T(8,128)(2,1)}, bf16[2304,384]{1,0:T(8,128)(2,1)}, u32[]{:S(2)}, u32[]{:S(2)}) collective-permute-start(bf16[2304,384]{1,0:T(8,128)(2,1)} %slice.499), channel_id=1, source_target_pairs={{0,16},{4,20},{8,24},{12,28},{16,0},{20,4},{24,8},{28,12},{1,17},{... | collective-permute-start | bytes 5308424 | tf_op jit(solution)/shard_map/ppermute | solution.py:21
  924.3 110.6 %collective-permute-start.85 = (bf16[2304,384]{1,0:T(8,128)(2,1)}, bf16[2304,384]{1,0:T(8,128)(2,1)}, u32[]{:S(2)}, u32[]{:S(2)}) collective-permute-start(bf16[2304,384]{1,0:T(8,128)(2,1)} %slice.493), channel_id=1, source_target_pairs={{0,8},{4,12},{8,0},{12,4},{16,24},{20,28},{24,16},{28,20},{1,9},{5... | collective-permute-start | bytes 5308424 | tf_op jit(solution)/shard_map/ppermute | solution.py:21
  961.3 79.3 %collective-permute-start.80 = (bf16[512,768]{1,0:T(8,128)(2,1)S(1)}, bf16[512,768]{1,0:T(8,128)(2,1)S(1)}, u32[]{:S(2)}, u32[]{:S(2)}) collective-permute-start(bf16[512,768]{1,0:T(8,128)(2,1)S(1)} %copy-done.97), channel_id=1, source_target_pairs={{0,2},{1,3},{2,0},{3,1},{4,6},{5,7},{6,4},{7,5},{8,10},{9,11},{10,... | collective-permute-start | bytes 2359304 | tf_op jit(solution)/shard_map/ppermute | solution.py:21
  1032.3 125.8 %collective-permute-start.96 = (bf16[576,768]{1,0:T(8,128)(2,1)S(1)}, bf16[576,768]{1,0:T(8,128)(2,1)S(1)}, u32[]{:S(2)}, u32[]{:S(2)}) collective-permute-start(bf16[576,768]{1,0:T(8,128)(2,1)S(1)} %split.819), channel_id=1, source_target_pairs={{0,1},{1,0},{2,3},{3,2},{4,5},{5,4},{6,7},{7,6},{8,9},{9,8},{10,11... | collective-permute-start | bytes 2654216 | tf_op jit(solution)/shard_map/ppermute | solution.py:21
  1034.9 124.7 %collective-permute-start.91 = (bf16[1152,384]{1,0:T(8,128)(2,1)S(1)}, bf16[1152,384]{1,0:T(8,128)(2,1)S(1)}, u32[]{:S(2)}, u32[]{:S(2)}) collective-permute-start(bf16[1152,384]{1,0:T(8,128)(2,1)S(1)} %split.811), channel_id=1, source_target_pairs={{0,2},{1,3},{2,0},{3,1},{4,6},{5,7},{6,4},{7,5},{8,10},{9,11},{10,... | collective-permute-start | bytes 2654216 | tf_op jit(solution)/shard_map/ppermute | solution.py:21
  1040.6 120.8 %collective-permute-start.86 = (bf16[1152,384]{1,0:T(8,128)(2,1)S(1)}, bf16[1152,384]{1,0:T(8,128)(2,1)S(1)}, u32[]{:S(2)}, u32[]{:S(2)}) collective-permute-start(bf16[1152,384]{1,0:T(8,128)(2,1)S(1)} %split.805), channel_id=1, source_target_pairs={{0,2},{1,3},{2,0},{3,1},{4,6},{5,7},{6,4},{7,5},{8,10},{9,11},{10,... | collective-permute-start | bytes 2654216 | tf_op jit(solution)/shard_map/ppermute | solution.py:21
  1047.4 93.7 %collective-permute-start.71 = (bf16[512,384]{1,0:T(8,128)(2,1)S(1)}, bf16[512,384]{1,0:T(8,128)(2,1)S(1)}, u32[]{:S(2)}, u32[]{:S(2)}) collective-permute-start(bf16[512,384]{1,0:T(8,128)(2,1)S(1)} %split.779), channel_id=1, source_target_pairs={{0,2},{1,3},{2,0},{3,1},{4,6},{5,7},{6,4},{7,5},{8,10},{9,11},{10,... | collective-permute-start | bytes 1179656 | tf_op jit(solution)/shard_map/ppermute | solution.py:21
  (232 other events, 6341.5 us)

commit v2 on v1

--- a/solution.py
+++ b/solution.py
@@ -14,6 +14,7 @@
 STEP = 16
 GELU_A = 0.7978845608028654
 GELU_B = 0.044715
+TINY = pl.CostEstimate(flops=1, bytes_accessed=1, transcendentals=0)
 
 
 def swap(values, axis_name, bit):
@@ -56,38 +57,90 @@
     return runs[0] if len(runs) == 1 else jnp.concatenate(runs, axis=1)
 
 
-def gather_matrix(unit, order):
-    held = [0]
-    for kind, bit in order:
-        other = swap(unit, *((("tp", bit)) if kind == "z" else ("fsdp", 2 * bit)))
-        if kind == "z":
-            unit = jnp.concatenate([unit, other], axis=0)
-            continue
-        width = unit.shape[1] // len(held)
-        parts = {j: unit[:, k * width : (k + 1) * width] for k, j in enumerate(held)}
-        parts |= {j ^ bit: other[:, k * width : (k + 1) * width] for k, j in enumerate(held)}
-        held = sorted(parts)
-        unit = jnp.concatenate([parts[j] for j in held], axis=1)
-    return unit
-
-
-def scatter_matrix(total, order, chips):
-    held = list(range(chips))
-    for step, (kind, bit) in enumerate(reversed(order)):
-        if kind == "z":
-            keep, send = jnp.split(total, 2, axis=0)
-            got = swap(send, "tp", bit)
+def after(value, *others):
+    return lax.optimization_barrier((value, *others))[0]
+
+
+def spread(pieces, bits):
+    for bit in bits:
+        held = sorted(pieces)
+        if len(held) <= 2:
+            got = {j ^ bit: swap(pieces[j], "fsdp", 2 * bit) for j in held}
         else:
-            at = {j: k for k, j in enumerate(held)}
-            count = len(held)
-            send = lane_blocks(total, count, [at[j] for j in held if j & bit])
-            keep = lane_blocks(total, count, [at[j] for j in held if not j & bit])
-            held = [j for j in held if not j & bit]
-            got = swap(send, "fsdp", 2 * bit)
-        total = keep.astype(F32) + got.astype(F32)
-        if step < len(order) - 1:
-            total = total.astype(BF)
-    return total
+            other = swap(jnp.concatenate([pieces[j] for j in held], axis=1), "fsdp", 2 * bit)
+            width = pieces[held[0]].shape[1]
+            got = {j ^ bit: other[:, k * width : (k + 1) * width] for k, j in enumerate(held)}
+        pieces = pieces | got
+    return pieces
+
+
+def finish(pieces, ahead, bits):
+    for bit in bits:
+        got = {j ^ bit: swap(v, "fsdp", 2 * bit) for j, v in pieces.items() if j ^ bit not in ahead}
+        pieces = pieces | ahead | got
+        ahead = {}
+    return pieces
+
+
+def fence(*groups):
+    return lax.optimization_barrier(groups)
+
+
+def join_kernel(half, counts, *refs):
+    out = refs[-1]
+    first, second = refs[: counts[0]], refs[counts[0] : -1]
+
+    def put(parts):
+        width = parts[0].shape[1]
+        for k, part in enumerate(parts):
+            out[:, k * width : (k + 1) * width] = part[...]
+
+    if not second:
+        put(first)
+        return
+    pl.when(pl.program_id(0) < half)(lambda: put(first))
+    pl.when(pl.program_id(0) >= half)(lambda: put(second))
+
+
+def join(pieces, start=0, count=None, below=None, below_start=0):
+    groups = [[p[j] for j in sorted(p)] for p in (pieces, below) if p is not None]
+    starts = [start, below_start]
+    count = groups[0][0].shape[0] - start if count is None else count
+    lanes = groups[0][0].shape[1]
+    block = max((b for b in range(16, 513, 16) if all(v % b == 0 for v in (count, *starts))), default=0)
+    if lanes % 128 or not block:
+        rows = [jnp.concatenate([v[at : at + count] for v in g], axis=1) for g, at in zip(groups, starts)]
+        return jnp.concatenate(rows, axis=0)
+    half = count // block
+    specs = []
+    for n, group in enumerate(groups):
+        first = starts[n] // block
+
+        def index(i, n=n, first=first):
+            return (first + jnp.clip(i - n * half, 0, half - 1), 0)
+
+        specs += [pl.BlockSpec((block, lanes), index)] * len(group)
+    flat_groups = [v for g in groups for v in g]
+    width = lanes * len(groups[0])
+    return pl.pallas_call(
+        functools.partial(join_kernel, half, [len(g) for g in groups]),
+        grid=(half * len(groups),),
+        in_specs=specs,
+        out_specs=pl.BlockSpec((block, width), lambda i: (i, 0)),
+        out_shape=jax.ShapeDtypeStruct((count * len(groups), width), flat_groups[0].dtype),
+        cost_estimate=TINY,
+        name="join",
+    )(*flat_groups)
+
+
+def shrink(total, held, bits):
+    for bit in reversed(bits):
+        at = {j: k for k, j in enumerate(held)}
+        send = lane_blocks(total, len(held), [at[j] for j in held if j & bit])
+        keep = lane_blocks(total, len(held), [at[j] for j in held if not j & bit])
+        held = [j for j in held if not j & bit]
+        total = (keep.astype(F32) + swap(send, "fsdp", 2 * bit).astype(F32)).astype(BF)
+    return total, held
 
 
 def minus_expm1(y):
@@ -201,11 +254,7 @@
             pltpu.VMEM((length, width), F32),
             pltpu.VMEM((length, width), F32),
         ],
-        cost_estimate=pl.CostEstimate(
-            flops=60 * branch.size + 4 * branch.size * width,
-            bytes_accessed=20 * branch.size,
-            transcendentals=4 * branch.size,
-        ),
+        cost_estimate=TINY,
         name="forward_scan",
     )(branch, halo, conv_w, vectors, rate_w, inlet_w)
 
@@ -261,9 +310,7 @@
         in_specs=[wide] * 4,
         out_specs=[wide] * 3,
         out_shape=[full(BF), full(F32), full(F32)],
-        cost_estimate=pl.CostEstimate(
-            flops=60 * state.size, bytes_accessed=24 * state.size, transcendentals=state.size
-        ),
+        cost_estimate=TINY,
         name="backward_scan",
     )(d_mixed, gate_pre, state, decay)
 
@@ -431,13 +478,106 @@
             pltpu.VMEM((length, width), BF),
             pltpu.VMEM((length + 8, width), F32),
         ],
-        cost_estimate=pl.CostEstimate(
-            flops=100 * branch.size + 12 * branch.size * width,
-            bytes_accessed=22 * branch.size,
-            transcendentals=5 * branch.size,
-        ),
+        cost_estimate=TINY,
         name="backward_gates",
     )(local_c, prod_c, carry_in, state, state_in, conv_out, branch, halo, conv_w, vectors, rate_w, inlet_w)
+
+
+def outer_kernel(values, cotangent, out):
+    out[...] = lax.dot_general(
+        values[...], cotangent[...], (((0,), (0,)), ((), ())), preferred_element_type=F32
+    ).astype(BF)
+
+
+def run_outer(values, cotangent):
+    values = values.reshape(-1, values.shape[-1])
+    cotangent = cotangent.reshape(-1, cotangent.shape[-1])
+    rows, channels = values.shape
+    width = cotangent.shape[1]
+    block = 256 if channels % 256 == 0 else channels
+    return pl.pallas_call(
+        outer_kernel,
+        grid=(channels // block,),
+        in_specs=[
+            pl.BlockSpec((rows, block), lambda i: (0, i)),
+            pl.BlockSpec((rows, width), lambda i: (0, 0)),
+        ],
+        out_specs=pl.BlockSpec((block, width), lambda i: (i, 0)),
+        out_shape=jax.ShapeDtypeStruct((channels, width), BF),
+        cost_estimate=TINY,
+        name="outer",
+    )(values, cotangent)
+
+
+def two_products_kernel(first, first_w, second, second_w, out):
+    total = jnp.dot(first[...], first_w[...], preferred_element_type=F32)
+    total = total + jnp.dot(second[...], second_w[...], preferred_element_type=F32)
+    out[...] = total.astype(BF)
+
+
+def run_two_products(first, first_w, second, second_w):
+    lead = first.shape[:-1]
+    inner = first.shape[-1]
+    first, second = first.reshape(-1, inner), second.reshape(-1, inner)
+    rows, width = first.shape[0], first_w.shape[1]
+    block = 256 if width % 256 == 0 else width
+    whole = pl.BlockSpec((rows, inner), lambda i: (0, 0))
+    column = pl.BlockSpec((inner, block), lambda i: (0, i))
+    total = pl.pallas_call(
+        two_products_kernel,
+        grid=(width // block,),
+        in_specs=[whole, column, whole, column],
+        out_specs=pl.BlockSpec((rows, block), lambda i: (0, i)),
+        out_shape=jax.ShapeDtypeStruct((rows, width), BF),
+        cost_estimate=TINY,
+        name="two_products",
+    )(first, first_w, second, second_w)
+    return total.reshape(*lead, width)
+
+
+def norm_back_kernel(values, gain, mine, other, direct, total, rounded, sums):
+    v = values[...]
+    inv_rms = lax.rsqrt(jnp.mean(v * v, axis=-1, keepdims=True) + EPS)
+    unit = v * inv_rms
+    cot = mine[...].astype(F32) + other[...].astype(F32)
+    scaled = cot * gain[...]
+    grad = inv_rms * (scaled - unit * jnp.mean(scaled * unit, axis=-1, keepdims=True))
+    found = direct[...] + grad
+    total[...] = found
+    rounded[...] = found.astype(BF)
+
+    @pl.when(pl.program_id(0) == 0)
+    def _():
+        sums[...] = jnp.zeros_like(sums)
+
+    part = cot * unit
+    fold = part[0:8]
+    for row in range(8, part.shape[0], 8):
+        fold = fold + part[row : row + 8]
+    sums[...] += fold
+
+
+def run_norm_back(values, gain_vec, mine, other, direct):
+    shape = values.shape
+    width = shape[-1]
+    values, mine, other, direct = (v.reshape(-1, width) for v in (values, mine, other, direct))
+    rows = values.shape[0]
+    block = 128
+    some = pl.BlockSpec((block, width), lambda i: (i, 0))
+    total, rounded, sums = pl.pallas_call(
+        norm_back_kernel,
+        grid=(rows // block,),
+        in_specs=[some, pl.BlockSpec((1, width), lambda i: (0, 0)), some, some, some],
+        out_specs=[some, some, pl.BlockSpec((8, width), lambda i: (0, 0))],
+        out_shape=[
+            jax.ShapeDtypeStruct(values.shape, F32),
+            jax.ShapeDtypeStruct(values.shape, BF),
+            jax.ShapeDtypeStruct((8, width), F32),
+        ],
+        cost_estimate=TINY,
+        name="norm_back",
+    )(values, gain_vec[None], mine, other, direct)
+    return total.reshape(shape), rounded.reshape(shape), jnp.sum(sums, axis=0)
 
 
 def rms_norm(values, gain_vec):
@@ -499,12 +639,19 @@
     width = rate_weight.shape[2]
     taps = conv_weight.shape[0]
 
-    zs = [("z", b) for b in bits_of(tp)]
-    ds = [("d", b) for b in bits_of(chips)]
-    order_a = zs + ds
-    order_b = zs + ds[::-1]
-    order_mid_a = ds[:1] + zs + ds[1:]
-    order_mid_b = ds[-1:] + zs + ds[:-1]
+    bits = bits_of(chips)
+    near, far = bits[: len(bits) // 2], bits[len(bits) // 2 :]
+    every = list(range(chips))
+
+    def block_order(some):
+        held = [0]
+        for bit in some:
+            held = sorted(held + [j ^ bit for j in held])
+        return held
+
+    lanes = 2 * model_width // fsdp
+    half_r = branch_weight.shape[1] // 2
+    half_f = geglu_gate.shape[1] // 2
 
     def same_chip(values):
         return swap(values, "fsdp", 1)
@@ -512,46 +659,57 @@
     def both_rows(values):
         return in_core_order(values, same_chip(values), core, 0)
 
-    def unit_of(matrix, channel_axis):
-        mine = pick_half(matrix, core, channel_axis)
-        other = same_chip(pick_half(matrix, 1 - core, channel_axis))
-        if channel_axis == 1:
-            mine, other = mine.T, other.T
-        return in_core_order(mine, other, core, 1)
+    def units(matrices):
+        def half(which):
+            parts = [pick_half(m, which, axis) for m, axis in matrices]
+            return jnp.concatenate([p.T if a == 1 else p for p, (_, a) in zip(parts, matrices)], axis=0)
+
+        return in_core_order(half(core), same_chip(half(1 - core)), core, 1)
 
     x4 = both_rows(inputs)
-    w_branch = gather_matrix(unit_of(branch_weight, 1), order_a)
-    w_gate = gather_matrix(unit_of(gate_weight, 1), order_b)
+    lengths4 = both_rows(seq_lengths)
+    count = jnp.broadcast_to(jnp.sum(lengths4.astype(F32)), (8, 128))
+    for b in bits:
+        count = count + swap(count, "fsdp", 2 * b)
+    valid_total = count[0, 0]
+    unit_r = units([(branch_weight, 1), (gate_weight, 1), (out_weight, 0)])
+    unit_f = units([(geglu_gate, 1), (geglu_up, 1), (geglu_down, 0)])
 
     rows_chip = 2 * rate_weight.shape[1]
+    pair_size = 2 * rows_chip * width
+    pair_lines = -(-pair_size // (16 * lanes)) * 16
     pair = jnp.concatenate([rate_weight, inlet_weight], axis=1)
-    pair_mine = pick_half(pair, core, 0)[0]
-    pair_other = same_chip(pick_half(pair, 1 - core, 0)[0])
-    pair_unit = in_core_order(
-        pair_mine.reshape(2, -1, width), pair_other.reshape(2, -1, width), core, 1
+    unit_p = in_core_order(
+        pick_half(pair, core, 0).reshape(2, -1, width),
+        same_chip(pick_half(pair, 1 - core, 0)).reshape(2, -1, width),
+        core,
+        1,
     )
-
-    def pack_pair(values):
-        return values.reshape(values.shape[0], -1)
-
-    held = pair_unit[None]
-    for b in bits_of(tp):
-        held = jnp.concatenate([held, swap(held, "tp", b)], axis=0)
-    held = held[:, :, None]
-    for b in bits_of(chips):
-        held = jnp.concatenate([held, swap(held, "fsdp", 2 * b)], axis=2)
-    held = xor_blocks(held, 2, chips, chip)
-    held = held.reshape(tp, 2, chips * rows_chip, width)
-    w_rate, w_inlet = held[:, 0], held[:, 1]
-
-    w_out = gather_matrix(unit_of(out_weight, 0), order_mid_b)
-    w_ffgate = gather_matrix(unit_of(geglu_gate, 1), order_a)
-    w_ffup = gather_matrix(unit_of(geglu_up, 1), order_b)
-    w_ffdown = gather_matrix(unit_of(geglu_down, 0), order_mid_a)
-
-    def to_relative(values):
-        return xor_blocks(values, values.ndim - 1, tp, z)
-
+    unit_p = jnp.pad(unit_p.reshape(-1), (0, pair_lines * lanes - pair_size)).reshape(pair_lines, lanes)
+
+    def all_z(values):
+        return lax.all_gather(values, "tp", axis=0, tiled=False)
+
+    def flat(values):
+        return values.reshape(-1, values.shape[-1])
+
+    top = tp // 2
+
+    def rows_of(gathered, start, count, blocks=slice(None)):
+        return flat(gathered[blocks, start : start + count])
+
+    first_z = all_z(jnp.concatenate([unit_r[: 2 * half_r], unit_p], axis=0))
+    second_z = all_z(after(unit_f[: 2 * half_f], first_z))
+    out_own = unit_r[2 * half_r :]
+    out_parts = {0: out_own} | {j: swap(out_own, "fsdp", 2 * j) for j in every[1:]}
+    first_z, x4, lengths4, valid_total, out_parts = fence(first_z, x4, lengths4, valid_total, out_parts)
+    a1 = jnp.concatenate([rows_of(first_z, 0, half_r), rows_of(first_z, 2 * half_r, pair_lines)], axis=0)
+    b1 = rows_of(first_z, half_r, half_r)
+    left_a, left_b = block_order(near), block_order(far)
+    a1, b1 = spread({0: a1}, near), spread({0: b1}, far)
+    first_a, first_b = a1[near[-1]], b1[far[-1]]
+    a1, b1 = spread(a1, far), spread(b1, near)
+    a3, b3 = {0: rows_of(second_z, 0, half_f)}, {0: rows_of(second_z, half_f, half_f)}
     local_vectors = jnp.concatenate(
         [
             conv_weight,
@@ -559,33 +717,41 @@
         ],
         axis=0,
     )
-    held = pick_half(local_vectors, core, 1)
+    held = pick_half(after(local_vectors, first_a, first_b), core, 1)
     for b in bits_of(tp):
         held = jnp.concatenate([held, swap(held, "tp", b)], axis=1)
+    held = xor_blocks(held, 1, tp, z)
+
+    def to_chip(values):
+        return xor_blocks(values, values.ndim - 1, chips, chip)
+
+    gain1, gain2 = to_chip(first_gain), to_chip(second_gain)
+    x4 = to_chip(x4)
+    residual = x4.astype(F32)
+    first_rows = rms_norm(residual, gain1).astype(BF)
+    a1, b1, a3, b3, held, first_rows = fence(a1, b1, a3, b3, held, first_rows)
+    out_z = all_z(after(join(out_parts), second_z, a1[0]))
+    third_z = all_z(after(unit_f[2 * half_f :], out_z))
+    a3, b3 = spread(a3, near), spread(b3, far)
+    far_a = {k ^ j: swap(a3[k], "fsdp", 2 * j) for k in [0] for j in far[:1]}
+    near_b = {k ^ j: swap(b3[k], "fsdp", 2 * j) for k in [0] for j in near[:1]}
+    size_r = tp * half_r
+    w_branch, w_gate = join(a1, 0, size_r), join(b1, 0, size_r)
+    w_out = flat(out_z)
+    w_pair = [a1[j][size_r : size_r + tp * pair_lines].reshape(tp, -1)[:, :pair_size] for j in every]
+    w_pair = jnp.stack(w_pair, axis=1).reshape(tp, chips, 2, rows_chip, width)
+    w_pair = xor_blocks(w_pair, 1, chips, chip).transpose(2, 0, 1, 3, 4).reshape(2, tp, chips * rows_chip, width)
+    w_rate, w_inlet = w_pair[0], w_pair[1]
+
     taps_w = held[:taps]
     b_branch, b_gate, b_conv, b_rate, b_inlet, decay_vec = (held[taps + k] for k in range(6))
     soft = jax.nn.softplus(-decay_vec)
     vectors = jnp.stack([b_conv, b_rate, b_inlet, soft])
 
-    lengths4 = both_rows(seq_lengths)
-    count = jnp.broadcast_to(jnp.sum(lengths4.astype(F32)), (8, 128))
-    for b in bits_of(chips):
-        count = count + swap(count, "fsdp", 2 * b)
-    valid_total = count[0, 0]
-
-    def to_chip(values):
-        return xor_blocks(values, values.ndim - 1, chips, chip)
-
-    gain1, gain2 = to_chip(first_gain), to_chip(second_gain)
-    x4 = to_chip(x4)
-    residual = x4.astype(F32)
-    first_rows = rms_norm(residual, gain1).astype(BF)
     branch_pre = times_t(first_rows, w_branch) + b_branch
-    gate_pre = times_t(first_rows, w_gate) + b_gate
 
     def along_z(values, shift):
-        pairs = [(i, i + shift) for i in range(tp) if 0 <= i + shift < tp]
-        return to_relative(lax.ppermute(to_relative(values), "tp", pairs))
+        return lax.ppermute(values, "tp", [(i, i + shift) for i in range(tp) if 0 <= i + shift < tp])
 
     halo = jnp.pad(along_z(branch_pre[:, local_len - taps + 1 :], 1), ((0, 0), (8 - taps + 1, 0), (0, 0)))
     conv_out, decay_rate, local_state, prod_decay = run_forward(
@@ -597,48 +763,98 @@
         got = along_z(ends, shift)
         state_in = got[1] + got[0] * state_in
     state_in = state_in[:, None]
+    state_in, a3, b3, far_a, near_b = fence(state_in, a3, b3, far_a, near_b)
+    gate_pre = times_t(after(first_rows, state_in), w_gate) + b_gate
+    a3, b3 = finish(a3, far_a, far), finish(b3, near_b, near)
     state = local_state + prod_decay * state_in
     mixed = (state * jax.nn.gelu(gate_pre)).astype(BF)
-
     def core_sum(term):
         return term.astype(F32) + same_chip(term).astype(F32)
 
-    middle = residual + core_sum(times(mixed, w_out, BF))
+    out_term, a3, b3, third_z = fence(times(mixed, w_out, BF), a3, b3, third_z)
+    a4, b4 = {0: flat(third_z[:top])}, {0: flat(third_z[top:])}
+    a4, b4 = spread(a4, near), spread(b4, far)
+    w_ffgate, w_ffup = join(a3), join(b3)
+    middle = residual + core_sum(out_term)
     second_rows = rms_norm(middle, gain2).astype(BF)
+    second_rows, a4, b4 = fence(second_rows, a4, b4)
+    a4, b4 = spread(a4, far), spread(b4, near)
+    teacher4 = both_rows(after(teacher, second_rows))
     ff_gate = times_t(second_rows, w_ffgate)
     ff_up = times_t(second_rows, w_ffup)
     ff_hidden = (jax.nn.gelu(ff_gate) * ff_up).astype(BF)
+    ff_hidden, a4, b4, teacher4 = fence(ff_hidden, a4, b4, teacher4)
+    w_ffdown = join(a4, 0, None, b4, 0)
     final = middle + core_sum(times(ff_hidden, w_ffdown, BF))
 
     positions = z * local_len + jnp.arange(local_len, dtype=jnp.int32)
     valid_mask = (positions[None, :] < lengths4[:, None]).astype(F32)[..., None]
-    teacher4 = to_chip(both_rows(teacher)).astype(F32)
+    teacher4 = to_chip(teacher4).astype(F32)
     mismatch = final - teacher4
     loss_part = jnp.sum(valid_mask * mismatch * mismatch)
     scaling = seq_dev * fsdp * full_len / valid_total
     out_cot = valid_mask * mismatch * scaling
     ff_cot = out_cot.astype(BF)
 
-    g_ffdown = scatter_matrix(outer_sum(ff_hidden, ff_cot), order_mid_a, chips)
+    def by_z(a, b):
+        return lax.psum_scatter(
+            jnp.concatenate([a.reshape(tp, -1, lanes), b.reshape(tp, -1, lanes)], axis=1),
+            "tp",
+            scatter_dimension=0,
+            tiled=False,
+        )
+
+    def halves(grad):
+        return jnp.split(grad, 2, axis=0)
+
+    def far_first(grad):
+        return shrink(grad, every, far)[0]
+
+    def near_first(grad):
+        return shrink(grad, every, near)[0]
+
+    def far_last(grad):
+        return shrink(grad, left_b, far)[0]
+
+    def near_last(grad):
+        return shrink(grad, left_a, near)[0]
+
+    ff_cot, g_ffdown = fence(ff_cot, outer_sum(ff_hidden, ff_cot))
+    down_sum = lax.psum_scatter(g_ffdown.reshape(tp, half_f, model_width), "tp", scatter_dimension=0, tiled=False)
     d_hidden = times_t(ff_cot, w_ffdown)
     act, slope = gelu_parts(ff_gate)
     d_up = (d_hidden * act).astype(BF)
     d_ffgate = (d_hidden * ff_up * slope).astype(BF)
-    g_ffgate = scatter_matrix(outer_sum(d_ffgate, second_rows), order_a, chips)
-    g_ffup = scatter_matrix(outer_sum(d_up, second_rows), order_b, chips)
-    d_second = core_sum((times(d_ffgate, w_ffgate) + times(d_up, w_ffup)).astype(BF))
-    d_mid_norm, g_second = norm_back(middle, gain2, d_second)
-    d_middle = out_cot + d_mid_norm
-    mid_cot = d_middle.astype(BF)
+    g_ffgate = run_outer(d_ffgate, second_rows)
+    d_ffgate, d_up, g_ffgate = fence(d_ffgate, d_up, g_ffgate)
+    top_g, low_g = halves(g_ffgate)
+    a3, b3 = far_first(top_g), near_first(low_g)
+    g_ffup = run_outer(d_up, second_rows)
+    d_second = run_two_products(d_ffgate, w_ffgate, after(d_up, g_ffup), w_ffup)
+    d_second, a3, b3, g_ffup = fence(d_second, a3, b3, g_ffup)
+    top_u, low_u = halves(g_ffup)
+    a6, b6 = far_first(top_u), near_first(low_u)
+    d_middle, mid_cot, g_second = run_norm_back(middle, gain2, d_second, same_chip(d_second), out_cot)
+    mid_cot, a3, b3, a6, b6 = fence(mid_cot, a3, b3, a6, b6)
+    a3, b3 = near_last(jnp.concatenate([a3, a6], axis=0)), far_last(jnp.concatenate([b3, b6], axis=0))
     d_mixed = times_t(mid_cot, w_out)
-    g_out = scatter_matrix(outer_sum(mixed, mid_cot), order_mid_b, chips)
     d_gate, local_c, prod_c = run_backward_scan(d_mixed, gate_pre, state, decay_rate, width)
+    d_gate, local_c, prod_c, a3, b3, down_sum = fence(d_gate, local_c, prod_c, a3, b3, down_sum)
+    unit_gu = jnp.concatenate([a3.reshape(2, -1, half_f, lanes), b3.reshape(2, -1, half_f, lanes)], axis=1)
+    unit_gu = unit_gu.transpose(1, 0, 2, 3).reshape(tp, -1, lanes)
+    unit_gu = lax.psum_scatter(unit_gu, "tp", scatter_dimension=0, tiled=False)
+    top_d, low_d = halves(down_sum)
+    a4, b4 = far_first(top_d), near_first(low_d)
     starts = jnp.stack([prod_c[:, 0], local_c[:, 0]]) * decay_rate[:, 0]
     carry_in = jnp.zeros_like(starts[0])
     for shift in reversed(range(1, tp)):
         got = along_z(starts, -shift)
         carry_in = got[1] + got[0] * carry_in
-    g_gate = scatter_matrix(outer_sum(d_gate, first_rows), order_b, chips)
+    g_out = outer_sum(after(mixed, d_gate), mid_cot)
+    g_gate = outer_sum(d_gate, first_rows)
+    local_c, g_gate, g_out, a4, b4 = fence(local_c, g_gate, g_out, a4, b4)
+    a4, b4 = near_last(a4), far_last(b4)
+    a2, b1 = far_first(g_out), near_first(g_gate)
     d_branch, head, tail, g_rate, g_inlet, sums = run_backward_gates(
         local_c,
         prod_c,
@@ -653,44 +869,53 @@
         w_rate,
         w_inlet,
     )
+    d_branch, head, a2, b1, a4, b4, unit_gu = fence(d_branch, head, a2, b1, a4, b4, unit_gu)
+    unit_d = jnp.concatenate([a4, b4], axis=0)
     ahead = along_z(head[:, : taps - 1], -1)
     edge = tail[:, 8 - taps + 1 :]
     for k in range(1, taps):
         first = taps - 1 - k
         edge = edge.at[:, first:].add(taps_w[k] * ahead[:, :k])
     d_branch = lax.dynamic_update_slice(d_branch, edge.astype(BF), (0, local_len - taps + 1, 0))
-    g_branch = scatter_matrix(outer_sum(d_branch, first_rows), order_a, chips)
+
+    a2, b1 = near_last(a2), far_last(b1)
+    g_branch = outer_sum(d_branch, first_rows)
+    g_rate, g_inlet, d_branch, a2, b1, g_branch = fence(g_rate, g_inlet, d_branch, a2, b1, g_branch)
+    unit_og = by_z(a2, b1)
+    top_b, low_b = halves(g_branch)
+    a1, b5 = far_first(top_b), near_first(low_b)
+    g_pair = jnp.stack([g_rate, g_inlet]).reshape(2, tp, chips, rows_chip, width)
+    g_pair = xor_blocks(g_pair, 2, chips, chip).astype(BF).transpose(1, 2, 0, 3, 4).reshape(tp, chips, -1)
+    g_pair = jnp.pad(g_pair, ((0, 0), (0, 0), (0, pair_lines * lanes - pair_size)))
+    g_pair = g_pair.reshape(tp, chips, pair_lines, lanes).transpose(0, 2, 1, 3).reshape(-1, model_width)
+    g_pair, a1, b5 = fence(g_pair, a1, b5)
+    top_p, low_p = halves(g_pair)
+    ap, bp = far_first(top_p), near_first(low_p)
+    a1, b5 = near_last(a1), far_last(b5)
     d_first_part = (times(d_branch, w_branch) + times(d_gate, w_gate)).astype(BF)
+    d_first_part, a1, b5, ap, bp, unit_og = fence(d_first_part, a1, b5, ap, bp, unit_og)
+    ap, bp = near_last(ap), far_last(bp)
+    unit_b = [jnp.concatenate(v, axis=0).reshape(tp, -1, lanes) for v in ((a1, b5), (ap, bp))]
+    unit_b = lax.psum_scatter(jnp.concatenate(unit_b, axis=1), "tp", scatter_dimension=0, tiled=False)
 
     def own(values):
         return pick_half(values, core, 0)
 
     d_first = own(d_first_part).astype(F32) + same_chip(pick_half(d_first_part, 1 - core, 0)).astype(F32)
-    d_in_norm, g_first = norm_back(inputs_rel := own(residual), gain1, d_first)
+    d_in_norm, g_first = norm_back(own(residual), gain1, d_first)
     input_grad = to_chip(own(d_middle) + d_in_norm)
     block_out = to_chip(own(final).astype(BF))
-
-    pair_g = jnp.stack([g_rate, g_inlet], axis=1).astype(BF)
-    pair_g = pair_g.reshape(tp, 2, chips, rows_chip, width)
-    pair_g = xor_blocks(pair_g, 2, chips, chip)
-    for b in reversed(bits_of(chips)):
-        keep, send = jnp.split(pair_g, 2, axis=2)
-        pair_g = (keep.astype(F32) + swap(send, "fsdp", 2 * b).astype(F32)).astype(BF)
-    for b in reversed(bits_of(tp)):
-        keep, send = jnp.split(pair_g, 2, axis=0)
-        pair_g = keep.astype(F32) + swap(send, "tp", b).astype(F32)
-        if b > 1:
-            pair_g = pair_g.astype(BF)
-    pair_g = pair_g.reshape(2, rows_chip, width)
-    pair_mine = pick_half(pair_g, core, 1)
-    pair_other = same_chip(pick_half(pair_g, 1 - core, 1))
-    pair_g = in_core_order(pair_mine[None], pair_other[None], core, 0)
 
     def to_own(grad, channel_axis):
         mine = pick_half(grad, core, 1)
         other = same_chip(pick_half(grad, 1 - core, 1))
         whole = in_core_order(mine, other, core, 0)
-        return whole.T if channel_axis == 1 else whole
+        return (whole.T if channel_axis == 1 else whole).astype(F32)
+
+    pair_g = unit_b[half_r:].reshape(-1)[:pair_size].reshape(2, rows_chip, width)
+    pair_g = in_core_order(
+        pick_half(pair_g, core, 1)[None], same_chip(pick_half(pair_g, 1 - core, 1))[None], core, 0
+    ).astype(F32)
 
     sums = jnp.sum(sums, axis=1)
     small = jnp.concatenate(
@@ -706,32 +931,32 @@
         ],
         axis=0,
     )
-    for b in bits_of(chips):
-        small = small + swap(small, "fsdp", 2 * b)
-    for b in reversed(bits_of(tp)):
-        keep, send = jnp.split(small, 2, axis=1)
-        small = keep + swap(send, "tp", b)
-    small = in_core_order(small, same_chip(small), core, 1)
-    stats = jnp.stack(
+    found = jnp.concatenate(
         [
-            jnp.broadcast_to(0.5 * loss_part, (model_width,)),
             to_chip(g_first),
             to_chip(0.5 * g_second),
+            jnp.broadcast_to(0.5 * loss_part, (128,)),
+            small.reshape(-1),
         ]
-    )
-    for b in bits_of(fsdp):
-        stats = stats + swap(stats, "fsdp", b)
+    ).reshape(-1, 128)
+    for b in bits:
+        found = found + swap(found, "fsdp", 2 * b)
     for b in bits_of(tp):
-        stats = stats + swap(stats, "tp", b)
-    loss_value = stats[0, 0] / (model_width * valid_total)
+        found = found + swap(found, "tp", b)
+    other = same_chip(found)
+    lines = (2 * model_width + 128) // 128
+    stats = (found[:lines] + other[:lines]).reshape(-1)
+    block = lambda v: lax.dynamic_index_in_dim(v[lines:].reshape(small.shape[0], tp, half_r), z, 1, keepdims=False)
+    small = in_core_order(block(found), block(other), core, 1)
+    loss_value = stats[2 * model_width] / (model_width * valid_total)
     return (
         block_out,
         loss_value,
         input_grad,
-        stats[1],
-        to_own(g_branch, 1),
+        stats[:model_width],
+        to_own(unit_b[:half_r], 1),
         small[0],
-        to_own(g_gate, 1),
+        to_own(unit_og[half_r:], 1),
         small[1],
         small[6:],
         small[5],
@@ -740,11 +965,11 @@
         pair_g[:, 1],
         small[4],
         small[2],
-        to_own(g_out, 0),
-        stats[2],
-        to_own(g_ffgate, 1),
-        to_own(g_ffup, 1),
-        to_own(g_ffdown, 0),
+        to_own(unit_og[:half_r], 0),
+        stats[model_width : 2 * model_width],
+        to_own(unit_gu[:half_f], 1),
+        to_own(unit_gu[half_f:], 1),
+        to_own(unit_d, 0),
     )
 
 

time: 1200 us -> 896 us (0.75)
  waiting for transfers between devices: 564 us -> 197 us
  Pallas kernels: 83.2 us -> 175 us
  matrix products: 216 us -> 140 us
  local copies, waits for them, and re-layouts: 76.1 us -> 117 us
  starting transfers between devices: 101 us -> 78.1 us
  between operations: 7.69 us -> 20.1 us
    ppermute x91 -> x69, waiting for transfers between devices: 553 us -> 149 us  [swap(): return lax.ppermute(values, axis_name, [(i, i ^ bit) for i in range(size)])]
    pallas_call x0 -> x10, Pallas kernels: none -> 91.9 us  [the longest x6 30.8 us: join(): pl.pallas_call(functools.partial(join_kernel, half, [len(g) for g in grou...]
    dot_general x6 -> x4, matrix products: 75.3 us -> 36.6 us  [times(): jnp.einsum('slk,kn->sln', values, matrix, preferred_element_type=dtype)]
    all_gather x0 -> x4, waiting for transfers between devices: none -> 35.8 us  [all_z(): return lax.all_gather(values, 'tp', axis=0, tiled=False)]
    convert_element_type x21 -> x31, other arithmetic: 23.6 us -> 55.3 us  [the longest x22 44.7 us: shrink(): (keep.astype(F32) + swap(send, 'fsdp', 2 * bit).astype(F32)).astype(BF)]
    dot_general x6 -> x4, matrix products: 55.8 us -> 24.9 us  [outer_sum(): jnp.einsum('slk,sln->kn', values, cotangent, preferred_element_type=F32)]
    ppermute x91 -> x69, starting transfers between devices: 84.7 us -> 58.3 us  [swap(): return lax.ppermute(values, axis_name, [(i, i ^ bit) for i in range(size)])]
    concatenate x20 -> x9, other arithmetic: 35 us -> 9.16 us  [the longest x1 2.41 us: shards(): jnp.concatenate([a3.reshape(2, -1, half_f, lanes), b3.reshape(2, -1, half...]
  transfers between devices with their start and end apart: 99 -> 85, of which waited for: 48 -> 38; matrix products, arithmetic and copies ran while one was open for 32% -> 39% of each run, Pallas kernels for 7% -> 19%
where the time goes in v2:
time: 896 us; the launch traced here: 884 us
  waiting for transfers between devices  197 us (22%)
  Pallas kernels  175 us (20%)
  other arithmetic  157 us (18%)
  matrix products  140 us (16%)
  local copies, waits for them, and re-layouts  117 us (13%)
  starting transfers between devices  78.1 us (9%)
  between operations  20.1 us (2%)
    ppermute x69, waiting for transfers between devices, swap(): return lax.ppermute(values, axis_name, [(i, i ^ bit) for i in range(size)])  149 us
    dot_general x6, matrix products, times_t(): jnp.einsum('sln,kn->slk', values, matrix, preferred_element_type=dtype)  78.1 us
    ppermute x69, starting transfers between devices, swap(): return lax.ppermute(values, axis_name, [(i, i ^ bit) for i in range(size)])  58.3 us
    convert_element_type x22, other arithmetic, shrink(): (keep.astype(F32) + swap(send, 'fsdp', 2 * bit).astype(F32)).astype(BF)  44.7 us
    pallas_call x1, Pallas kernels, run_backward_gates(): pl.pallas_call(backward_gates_kernel, grid=(channels // width, seqs), in_...  37.8 us
    dot_general x4, matrix products, times(): jnp.einsum('slk,kn->sln', values, matrix, preferred_element_type=dtype)  36.6 us
    all_gather x4, waiting for transfers between devices, all_z(): return lax.all_gather(values, 'tp', axis=0, tiled=False)  35.8 us
    pallas_call x6, Pallas kernels, join(): pl.pallas_call(functools.partial(join_kernel, half, [len(g) for g in grou...  30.8 us
  transfers between devices with their start and end apart: 85, of which 38 were waited for; matrix products, arithmetic and copies ran while one was open for 39% of the time, Pallas kernels for 19%

profile of v2, /device:TPU:0, one launch (start us, length us, event | category | flops | bytes accessed | tf_op | source)
XLA Modules:
  0.0 883.8 jit_solution(4618743776135088519)
XLA Ops:
  30.8 29.6 %all-gather.9.cloned.1.call-done = bf16[2432,384]{1,0:T(8,128)(2,1)} async-done(((bf16[608,384]{1,0:T(8,128)(2,1)}), bf16[2432,384]{1,0:T(8,128)(2,1)}) %all-gather.9.cloned.1.call-update) | async-done | bytes 1867792 | tf_op jit(solution)/shard_map/all_gather | solution.py:691
  92.5 14.4 %collective-permute-done.13.refs_2_ = bf16[1024,384]{1,0:T(8,128)(2,1)} collective-permute-done((bf16[1024,384]{1,0:T(8,128)(2,1)}, bf16[1024,384]{1,0:T(8,128)(2,1)}, u32[]{:S(2)}, u32[]{:S(2)}) %collective-permute-start.13) | collective-permute-done | bytes 786464 | tf_op jit(solution)/shard_map/ppermute | solution.py:22
  188.7 27.5 %forward_scan.1 = (bf16[4,256,1024]{2,1,0:T(8,128)(2,1)}, f32[4,256,1024]{2,1,0:T(8,128)}, f32[4,256,1024]{2,1,0:T(8,128)}, f32[4,256,1024]{2,1,0:T(8,128)}) custom-call(f32[4,256,1024]{2,1,0:T(8,128)} %copy-done.5, f32[4,8,1024]{2,1,0:T(8,128)} %pad.20.halo, f32[4,1024]{1,0:T(4,128)} %slice.528.conv_w, f32[4,1024]{1,0:T(4,128)} %pad_maximum_fusion.31.vectors, ...), custom_call_target="tpu_custom_call" | custom-call | flops 1 | bytes 1 | tf_op jit(solution)/shard_map/forward_scan/pallas_call | solution.py:239
  225.6 8.2 collective-permute-start.19
  240.0 13.9 %fusion.35 = (bf16[4,256,1024]{2,1,0:T(8,128)(2,1)}, f32[4,256,1024]{2,1,0:T(8,128)}, f32[4,256,1024]{2,1,0:T(8,128)}) fusion(f32[4,256,1024]{2,1,0:T(8,128)} %get-tuple-element.197, f32[4,256,1024]{2,1,0:T(8,128)} %get-tuple-element.198, f32[4,1024]{1,0:T(4,128)S(1)} %bitcast.293, f32[1024]{0:T(1024)S(1)} %bitcast.296, ...), kind=kOutput, calls=%fused_computation.55 | convolution fusion | flops 3234856960 | bytes 25186304 | tf_op jit(solution)/shard_map/sln,kn->slk/dot_general | solution.py:601
  253.9 7.6 fusion.39
  261.5 12.6 %collective-permute-done.26.refs_3_ = bf16[2304,384]{1,0:T(8,128)(2,1)} collective-permute-done((bf16[2304,384]{1,0:T(8,128)(2,1)}, bf16[2304,384]{1,0:T(8,128)(2,1)}, u32[]{:S(2)}, u32[]{:S(2)}) %collective-permute-start.26) | collective-permute-done | bytes 1769504 | tf_op jit(solution)/shard_map/ppermute | solution.py:22
  285.5 7.3 join.10.second_w
  304.3 9.9 %fusion.24 = f32[4,256,2304]{2,1,0:T(8,128)} fusion(bf16[4,256,1536]{2,1,0:T(8,128)(2,1)S(1)} %multiply_convert_fusion.1, bf16[2304,1536]{1,0:T(8,128)(2,1)S(1)} %copy-done.4), kind=kOutput, calls=%fused_computation.32 | convolution fusion | flops 7247757312 | bytes 19660800 | tf_op jit(solution)/shard_map/sln,kn->slk/dot_general | solution.py:601
  314.2 16.2 %fusion.8 = (bf16[4,256,2304]{2,1,0:T(8,128)(2,1)}, f32[4,256,2304]{2,1,0:T(8,128)}) fusion(f32[4,256,2304]{2,1,0:T(8,128)} %fusion.24, bf16[4,256,1536]{2,1,0:T(8,128)(2,1)S(1)} %multiply_convert_fusion.1, bf16[2304,1536]{1,0:T(8,128)(2,1)} %join.10.second_w), kind=kOutput, calls=%fused_computation.12 | convolution fusion | flops 7271350272 | bytes 33816576 | tf_op jit(solution)/shard_map/sln,kn->slk/dot_general | solution.py:601
  342.5 7.6 join.11
  350.1 12.3 %fusion.20 = bf16[4,256,1536]{2,1,0:T(8,128)(2,1)} fusion(bf16[4,256,2304]{2,1,0:T(8,128)(2,1)} %get-tuple-element.235, bf16[2304,1536]{1,0:T(8,128)(2,1)} %join.11), kind=kOutput, calls=%fused_computation.28 | convolution fusion | flops 7247757312 | bytes 14942208 | tf_op jit(solution)/shard_map/slk,kn->sln/dot_general | solution.py:597
  379.3 9.4 %bitcast_convert_fusion = bf16[2304,1536]{1,0:T(8,128)(2,1)} fusion(bf16[4,256,2304]{2,1,0:T(8,128)(2,1)S(1)} %bitcast.313, bf16[4,256,1536]{2,1,0:T(8,128)(2,1)S(1)} %get-tuple-element.247), kind=kOutput, calls=%fused_computation | convolution fusion | flops 7251296256 | bytes 14942208 | tf_op jit(solution)/shard_map/slk,sln->kn/dot_general | solution.py:605
  388.7 23.5 %multiply_convert_fusion = (bf16[4,256,2304]{2,1,0:T(8,128)(2,1)}, bf16[4,256,2304]{2,1,0:T(8,128)(2,1)}) fusion(f32[4,256,2304]{2,1,0:T(8,128)} %fusion.24, f32[4,256,2304]{2,1,0:T(8,128)} %get-tuple-element.533, bf16[4,256,1536]{2,1,0:T(8,128)(2,1)} %copy-done.21, bf16[2304,1536]{1,0:T(8,128)(2,1)} %join.11), kind=kOutput, calls=%fused_computation.22 | convolution fusion | flops 7299661824 | bytes 38535168 | tf_op jit(solution)/shard_map/sln,kn->slk/dot_general | solution.py:601
  412.3 13.4 %outer.2 = bf16[2304,1536]{1,0:T(8,128)(2,1)} custom-call(bf16[1024,2304]{1,0:T(8,128)(2,1)} %bitcast.230, bf16[1024,1536]{1,0:T(8,128)(2,1)} %bitcast.225), custom_call_target="tpu_custom_call" | custom-call | flops 1 | bytes 1 | tf_op jit(solution)/shard_map/outer/pallas_call | solution.py:498
  436.2 13.4 %outer.3 = bf16[2304,1536]{1,0:T(8,128)(2,1)} custom-call(bf16[1024,2304]{1,0:T(8,128)(2,1)} %bitcast.228, bf16[1024,1536]{1,0:T(8,128)(2,1)} %bitcast.226), custom_call_target="tpu_custom_call" | custom-call | flops 1 | bytes 1 | tf_op jit(solution)/shard_map/outer/pallas_call | solution.py:498
  449.6 21.1 %two_products.1 = bf16[1024,1536]{1,0:T(8,128)(2,1)} custom-call(bf16[1024,2304]{1,0:T(8,128)(2,1)} %bitcast.231, bf16[2304,1536]{1,0:T(8,128)(2,1)} %join.9.first_w, bf16[1024,2304]{1,0:T(8,128)(2,1)} %bitcast.229, bf16[2304,1536]{1,0:T(8,128)(2,1)} %join.10.second_w), custom_call_target="tpu_custom_call" | custom-call | flops 1 | bytes 1 | tf_op jit(solution)/shard_map/two_products/pallas_call | solution.py:526
  489.6 33.6 %collective-permute-done.41 = bf16[1152,768]{1,0:T(8,128)(2,1)} collective-permute-done((bf16[1152,768]{1,0:T(8,128)(2,1)}, bf16[1152,768]{1,0:T(8,128)(2,1)}, u32[]{:S(2)}, u32[]{:S(2)}) %collective-permute-start.41) | collective-permute-done | bytes 1769504 | tf_op jit(solution)/shard_map/ppermute | solution.py:22
  528.9 13.2 %norm_back.1 = (f32[1024,1536]{1,0:T(8,128)}, bf16[1024,1536]{1,0:T(8,128)(2,1)}, f32[8,1536]{1,0:T(8,128)}) custom-call(f32[1024,1536]{1,0:T(8,128)} %bitcast.224, f32[1,1536]{1,0:T(1,128)} %broadcast_in_dim.7.gain, bf16[1024,1536]{1,0:T(8,128)(2,1)} %bitcast.49.mine, bf16[1024,1536]{1,0:T(8,128)(2,1)} %bitcast.50.other, f32[1024,1536]{1,0:T(8,128)} %bitcast.227), custom_call_target="tpu_custom_call" | custom-call | flops 1 | bytes 1 | tf_op jit(solution)/shard_map/norm_back/pallas_call | solution.py:567
  557.7 8.3 fusion.37.d_mixed
  565.9 17.9 %backward_scan.1 = (bf16[4,256,1024]{2,1,0:T(8,128)(2,1)}, f32[4,256,1024]{2,1,0:T(8,128)}, f32[4,256,1024]{2,1,0:T(8,128)}) custom-call(f32[4,256,1024]{2,1,0:T(8,128)} %fusion.37.d_mixed, f32[4,256,1024]{2,1,0:T(8,128)} %get-tuple-element.531.gate_pre, f32[4,256,1024]{2,1,0:T(8,128)} %get-tuple-element.390.state, f32[4,256,1024]{2,1,0:T(8,128)} %get-tuple-element.258.decay), custom_call_target="tpu_custom_call" | custom-call | flops 1 | bytes 1 | tf_op jit(solution)/shard_map/backward_scan/pallas_call | solution.py:307
  656.6 37.8 %backward_gates.1 = (bf16[4,256,1024]{2,1,0:T(8,128)(2,1)}, f32[4,8,1024]{2,1,0:T(8,128)}, f32[4,8,1024]{2,1,0:T(8,128)}, f32[4,256,256]{2,1,0:T(8,128)}, f32[4,256,256]{2,1,0:T(8,128)}, /*index=5*/f32[8,8,1024]{2,1,0:T(8,128)}) custom-call(f32[4,256,1024]{2,1,0:T(8,128)} %get-tuple-element.271.local_c, f32[4,256,1024]{2,1,0:T(8,128)} %get-tuple-element.272.prod_c, ...), custom_call_target="tpu_custom_call" | custom-call | flops 1 | bytes 1 | tf_op jit(solution)/shard_map/backward_gates/pallas_call | solution.py:439
  724.4 7.8 bitcast_convert_fusion.1
  762.5 9.6 %add_convert_fusion = bf16[4,256,1536]{2,1,0:T(8,128)(2,1)} fusion(f32[4,256,1536]{2,1,0:T(8,128)} %fusion.44, bf16[4,256,1024]{2,1,0:T(8,128)(2,1)} %get-tuple-element.268, bf16[1024,1536]{1,0:T(8,128)(2,1)} %join.7), kind=kOutput, calls=%fused_computation.38 | convolution fusion | flops 3224371200 | bytes 14680064 | tf_op jit(solution)/shard_map/slk,kn->sln/dot_general | solution.py:597
  (600 shorter events, 487.7 us)
Async XLA Ops:
  7.2 53.2 %all-gather.9.cloned.1.call-start = ((), (), s32[]{:S(2)}) async-start(), calls=%async_computation.8 | async-start | bytes 2334720 | tf_op jit(solution)/shard_map/all_gather | solution.py:691
  16.0 116.7 %all-gather.11.cloned.1.call-start = ((), (), s32[]{:S(2)}) async-start(), calls=%async_computation.9 | async-start | bytes 4423680 | tf_op jit(solution)/shard_map/all_gather | solution.py:691
  23.1 52.7 %collective-permute-start.2 = (bf16[2,256,1536]{2,1,0:T(8,128)(2,1)S(1)}, bf16[2,256,1536]{2,1,0:T(8,128)(2,1)}, u32[]{:S(2)}, u32[]{:S(2)}) collective-permute-start(bf16[2,256,1536]{2,1,0:T(8,128)(2,1)S(1)} %copy-done.36), channel_id=1, source_target_pairs={{0,4},{4,0},{8,12},{12,8},{16,20},{20,16},{24,28},{28,24},{1,5},{5... | collective-permute-start | bytes 4718600 | tf_op jit(solution)/shard_map/ppermute | solution.py:22
  60.4 193.4 %all-gather.13.cloned.1.call-start = ((), (), s32[]{:S(2)}) async-start(), calls=%async_computation.10 | async-start | bytes 3932160 | tf_op jit(solution)/shard_map/all_gather | solution.py:691
  87.0 49.8 %collective-permute-start.10 = (bf16[1408,384]{1,0:T(8,128)(2,1)}, bf16[1408,384]{1,0:T(8,128)(2,1)}, u32[]{:S(2)}, u32[]{:S(2)}) collective-permute-start(bf16[1408,384]{1,0:T(8,128)(2,1)} %pad_maximum_fusion.11.refs_0_), channel_id=1, source_target_pairs={{0,16},{4,20},{8,24},{12,28},{16,0},{20,4},{24,8},{28,12},{1,17},{... | collective-permute-start | bytes 3244040 | tf_op jit(solution)/shard_map/ppermute | solution.py:22
  88.2 48.6 %collective-permute-start.12 = (bf16[1024,384]{1,0:T(8,128)(2,1)}, bf16[1024,384]{1,0:T(8,128)(2,1)}, u32[]{:S(2)}, u32[]{:S(2)}) collective-permute-start(bf16[1024,384]{1,0:T(8,128)(2,1)} %bitcast.10.refs_0_), channel_id=1, source_target_pairs={{0,8},{4,12},{8,0},{12,4},{16,24},{20,28},{24,16},{28,20},{1,9},{5... | collective-permute-start | bytes 2359304 | tf_op jit(solution)/shard_map/ppermute | solution.py:22
  149.1 112.4 %all-gather.15.cloned.1.call-start = ((), (), s32[]{:S(2)}) async-start(), calls=%async_computation.11 | async-start | bytes 2211840 | tf_op jit(solution)/shard_map/all_gather | solution.py:691
  151.1 446.1 %reduce-scatter.5.cloned.1.call-start = ((), (), s32[]{:S(2)}) async-start(), calls=%async_computation.4 | async-start | bytes 8847360 | tf_op jit(solution)/shard_map/reduce_scatter | solution.py:823
  160.8 76.2 %collective-permute-start.22 = (bf16[2304,384]{1,0:T(8,128)(2,1)}, bf16[2304,384]{1,0:T(8,128)(2,1)}, u32[]{:S(2)}, u32[]{:S(2)}) collective-permute-start(bf16[2304,384]{1,0:T(8,128)(2,1)} %bitcast.237), channel_id=1, source_target_pairs={{0,8},{4,12},{8,0},{12,4},{16,24},{20,28},{24,16},{28,20},{1,9},{5... | collective-permute-start | bytes 5308424 | tf_op jit(solution)/shard_map/ppermute | solution.py:22
  161.9 76.6 %collective-permute-start.24 = (bf16[2304,384]{1,0:T(8,128)(2,1)}, bf16[2304,384]{1,0:T(8,128)(2,1)}, u32[]{:S(2)}, u32[]{:S(2)}) collective-permute-start(bf16[2304,384]{1,0:T(8,128)(2,1)} %bitcast.238), channel_id=1, source_target_pairs={{0,16},{4,20},{8,24},{12,28},{16,0},{20,4},{24,8},{28,12},{1,17},{... | collective-permute-start | bytes 5308424 | tf_op jit(solution)/shard_map/ppermute | solution.py:22
  162.4 76.1 %collective-permute-start.23 = (bf16[2304,384]{1,0:T(8,128)(2,1)}, bf16[2304,384]{1,0:T(8,128)(2,1)}, u32[]{:S(2)}, u32[]{:S(2)}) collective-permute-start(bf16[2304,384]{1,0:T(8,128)(2,1)} %bitcast.234), channel_id=1, source_target_pairs={{0,16},{4,20},{8,24},{12,28},{16,0},{20,4},{24,8},{28,12},{1,17},{... | collective-permute-start | bytes 5308424 | tf_op jit(solution)/shard_map/ppermute | solution.py:22
  163.9 74.6 %collective-permute-start.25 = (bf16[2304,384]{1,0:T(8,128)(2,1)}, bf16[2304,384]{1,0:T(8,128)(2,1)}, u32[]{:S(2)}, u32[]{:S(2)}) collective-permute-start(bf16[2304,384]{1,0:T(8,128)(2,1)} %bitcast.235), channel_id=1, source_target_pairs={{0,8},{4,12},{8,0},{12,4},{16,24},{20,28},{24,16},{28,20},{1,9},{5... | collective-permute-start | bytes 5308424 | tf_op jit(solution)/shard_map/ppermute | solution.py:22
  388.7 319.3 %reduce-scatter.7.cloned.1.call-start = ((), (), s32[]{:S(2)}) async-start(), calls=%async_computation.5 | async-start | bytes 4423680 | tf_op jit(solution)/shard_map/reduce_scatter | solution.py:845
  430.7 40.8 %collective-permute-start.38 = (bf16[1152,768]{1,0:T(8,128)(2,1)}, bf16[1152,768]{1,0:T(8,128)(2,1)}, u32[]{:S(2)}, u32[]{:S(2)}) collective-permute-start(bf16[1152,768]{1,0:T(8,128)(2,1)} %pad_maximum_fusion.6), channel_id=1, source_target_pairs={{0,8},{4,12},{8,0},{12,4},{16,24},{20,28},{24,16},{28,20},{1,9},{5... | collective-permute-start | bytes 5308424 | tf_op jit(solution)/shard_map/ppermute | solution.py:22
  434.4 40.9 %collective-permute-start.37 = (bf16[1152,768]{1,0:T(8,128)(2,1)}, bf16[1152,768]{1,0:T(8,128)(2,1)}, u32[]{:S(2)}, u32[]{:S(2)}) collective-permute-start(bf16[1152,768]{1,0:T(8,128)(2,1)} %slice.554), channel_id=1, source_target_pairs={{0,16},{4,20},{8,24},{12,28},{16,0},{20,4},{24,8},{28,12},{1,17},{... | collective-permute-start | bytes 5308424 | tf_op jit(solution)/shard_map/ppermute | solution.py:22
  479.0 49.9 %collective-permute-start.39 = (bf16[4,256,1536]{2,1,0:T(8,128)(2,1)}, bf16[4,256,1536]{2,1,0:T(8,128)(2,1)}, u32[]{:S(2)}, u32[]{:S(2)}) collective-permute-start(bf16[4,256,1536]{2,1,0:T(8,128)(2,1)} %bitcast.48), channel_id=1, source_target_pairs={{0,4},{4,0},{8,12},{12,8},{16,20},{20,16},{24,28},{28,24},{1,5},{5... | collective-permute-start | bytes 9437192 | tf_op jit(solution)/shard_map/ppermute | solution.py:22
  481.9 41.3 %collective-permute-start.41 = (bf16[1152,768]{1,0:T(8,128)(2,1)}, bf16[1152,768]{1,0:T(8,128)(2,1)}, u32[]{:S(2)}, u32[]{:S(2)}) collective-permute-start(bf16[1152,768]{1,0:T(8,128)(2,1)} %pad_maximum_fusion.7), channel_id=1, source_target_pairs={{0,8},{4,12},{8,0},{12,4},{16,24},{20,28},{24,16},{28,20},{1,9},{5... | collective-permute-start | bytes 5308424 | tf_op jit(solution)/shard_map/ppermute | solution.py:22
  484.3 42.1 %collective-permute-start.40 = (bf16[1152,768]{1,0:T(8,128)(2,1)}, bf16[1152,768]{1,0:T(8,128)(2,1)}, u32[]{:S(2)}, u32[]{:S(2)}) collective-permute-start(bf16[1152,768]{1,0:T(8,128)(2,1)} %slice.560), channel_id=1, source_target_pairs={{0,16},{4,20},{8,24},{12,28},{16,0},{20,4},{24,8},{28,12},{1,17},{... | collective-permute-start | bytes 5308424 | tf_op jit(solution)/shard_map/ppermute | solution.py:22
  601.7 215.3 %reduce-scatter.9.cloned.1.call-start = ((), (), s32[]{:S(2)}) async-start(), calls=%async_computation.6 | async-start | bytes 1966080 | tf_op jit(solution)/shard_map/reduce_scatter | solution.py:800
  637.2 64.4 %collective-permute-start.50 = (bf16[1024,768]{1,0:T(8,128)(2,1)}, bf16[1024,768]{1,0:T(8,128)(2,1)}, u32[]{:S(2)}, u32[]{:S(2)}) collective-permute-start(bf16[1024,768]{1,0:T(8,128)(2,1)} %pad_maximum_fusion.9), channel_id=1, source_target_pairs={{0,8},{4,12},{8,0},{12,4},{16,24},{20,28},{24,16},{28,20},{1,9},{5... | collective-permute-start | bytes 4718600 | tf_op jit(solution)/shard_map/ppermute | solution.py:22
  640.5 64.4 %collective-permute-start.49 = (bf16[1024,768]{1,0:T(8,128)(2,1)}, bf16[1024,768]{1,0:T(8,128)(2,1)}, u32[]{:S(2)}, u32[]{:S(2)}) collective-permute-start(bf16[1024,768]{1,0:T(8,128)(2,1)} %slice.585), channel_id=1, source_target_pairs={{0,16},{4,20},{8,24},{12,28},{16,0},{20,4},{24,8},{28,12},{1,17},{... | collective-permute-start | bytes 4718600 | tf_op jit(solution)/shard_map/ppermute | solution.py:22
  654.7 44.0 %collective-permute-start.51 = (bf16[288,384]{1,0:T(8,128)(2,1)S(1)}, bf16[288,384]{1,0:T(8,128)(2,1)}, u32[]{:S(2)}, u32[]{:S(2)}) collective-permute-start(bf16[288,384]{1,0:T(8,128)(2,1)S(1)} %slice.591), channel_id=1, source_target_pairs={{0,8},{4,12},{8,0},{12,4},{16,24},{20,28},{24,16},{28,20},{1,9},{5... | collective-permute-start | bytes 663560 | tf_op jit(solution)/shard_map/ppermute | solution.py:22
  656.6 43.2 %collective-permute-start.52 = (bf16[288,384]{1,0:T(8,128)(2,1)}, bf16[288,384]{1,0:T(8,128)(2,1)}, u32[]{:S(2)}, u32[]{:S(2)}) collective-permute-start(bf16[288,384]{1,0:T(8,128)(2,1)} %slice.593), channel_id=1, source_target_pairs={{0,16},{4,20},{8,24},{12,28},{16,0},{20,4},{24,8},{28,12},{1,17},{... | collective-permute-start | bytes 663560 | tf_op jit(solution)/shard_map/ppermute | solution.py:22
  762.4 107.8 %reduce-scatter.11.cloned.1.call-start = ((), (), s32[]{:S(2)}) async-start(), calls=%async_computation.7 | async-start | bytes 1351680 | tf_op jit(solution)/shard_map/reduce_scatter | solution.py:899
  (135 other events, 1642.6 us)
Sparse Core Ops, SparseCore 0:
  16.1 44.2 all-gather.8
  62.5 70.0 all-gather.10
  149.2 60.9 all-gather.12
  212.2 40.0 all-gather.14
  388.8 122.7 reduce-scatter.4
  601.9 67.2 reduce-scatter.6
  762.5 35.1 reduce-scatter.8
  835.7 30.1 reduce-scatter.10

commit v3 on v2

--- a/solution.py
+++ b/solution.py
@@ -835,14 +835,12 @@
     top_u, low_u = halves(g_ffup)
     a6, b6 = far_first(top_u), near_first(low_u)
     d_middle, mid_cot, g_second = run_norm_back(middle, gain2, d_second, same_chip(d_second), out_cot)
-    mid_cot, a3, b3, a6, b6 = fence(mid_cot, a3, b3, a6, b6)
-    a3, b3 = near_last(jnp.concatenate([a3, a6], axis=0)), far_last(jnp.concatenate([b3, b6], axis=0))
+    mid_cot, a3, b3 = fence(mid_cot, a3, b3)
+    a3, b3 = near_last(a3), far_last(b3)
     d_mixed = times_t(mid_cot, w_out)
     d_gate, local_c, prod_c = run_backward_scan(d_mixed, gate_pre, state, decay_rate, width)
-    d_gate, local_c, prod_c, a3, b3, down_sum = fence(d_gate, local_c, prod_c, a3, b3, down_sum)
-    unit_gu = jnp.concatenate([a3.reshape(2, -1, half_f, lanes), b3.reshape(2, -1, half_f, lanes)], axis=1)
-    unit_gu = unit_gu.transpose(1, 0, 2, 3).reshape(tp, -1, lanes)
-    unit_gu = lax.psum_scatter(unit_gu, "tp", scatter_dimension=0, tiled=False)
+    d_gate, local_c, prod_c, a3, b3, a6, b6, down_sum = fence(d_gate, local_c, prod_c, a3, b3, a6, b6, down_sum)
+    a6, b6 = near_last(a6), far_last(b6)
     top_d, low_d = halves(down_sum)
     a4, b4 = far_first(top_d), near_first(low_d)
     starts = jnp.stack([prod_c[:, 0], local_c[:, 0]]) * decay_rate[:, 0]
@@ -852,7 +850,11 @@
         carry_in = got[1] + got[0] * carry_in
     g_out = outer_sum(after(mixed, d_gate), mid_cot)
     g_gate = outer_sum(d_gate, first_rows)
-    local_c, g_gate, g_out, a4, b4 = fence(local_c, g_gate, g_out, a4, b4)
+    local_c, g_gate, g_out, a4, b4, a6, b6 = fence(local_c, g_gate, g_out, a4, b4, a6, b6)
+    gate_sum = jnp.concatenate([a3, b3], axis=0).reshape(tp, -1, lanes)
+    up_sum = jnp.concatenate([a6, b6], axis=0).reshape(tp, -1, lanes)
+    unit_gu = jnp.concatenate([gate_sum, up_sum], axis=1)
+    unit_gu = lax.psum_scatter(unit_gu, "tp", scatter_dimension=0, tiled=False)
     a4, b4 = near_last(a4), far_last(b4)
     a2, b1 = far_first(g_out), near_first(g_gate)
     d_branch, head, tail, g_rate, g_inlet, sums = run_backward_gates(
@@ -869,7 +871,7 @@
         w_rate,
         w_inlet,
     )
-    d_branch, head, a2, b1, a4, b4, unit_gu = fence(d_branch, head, a2, b1, a4, b4, unit_gu)
+    d_branch, head, a2, b1, a4, b4 = fence(d_branch, head, a2, b1, a4, b4)
     unit_d = jnp.concatenate([a4, b4], axis=0)
     ahead = along_z(head[:, : taps - 1], -1)
     edge = tail[:, 8 - taps + 1 :]
@@ -880,7 +882,9 @@
 
     a2, b1 = near_last(a2), far_last(b1)
     g_branch = outer_sum(d_branch, first_rows)
-    g_rate, g_inlet, d_branch, a2, b1, g_branch = fence(g_rate, g_inlet, d_branch, a2, b1, g_branch)
+    g_rate, g_inlet, d_branch, a2, b1, g_branch, unit_gu = fence(
+        g_rate, g_inlet, d_branch, a2, b1, g_branch, unit_gu
+    )
     unit_og = by_z(a2, b1)
     top_b, low_b = halves(g_branch)
     a1, b5 = far_first(top_b), near_first(low_b)
@@ -888,7 +892,7 @@
     g_pair = xor_blocks(g_pair, 2, chips, chip).astype(BF).transpose(1, 2, 0, 3, 4).reshape(tp, chips, -1)
     g_pair = jnp.pad(g_pair, ((0, 0), (0, 0), (0, pair_lines * lanes - pair_size)))
     g_pair = g_pair.reshape(tp, chips, pair_lines, lanes).transpose(0, 2, 1, 3).reshape(-1, model_width)
-    g_pair, a1, b5 = fence(g_pair, a1, b5)
+    g_pair, a1, b5, d_branch = fence(g_pair, a1, b5, d_branch)
     top_p, low_p = halves(g_pair)
     ap, bp = far_first(top_p), near_first(low_p)
     a1, b5 = near_last(a1), far_last(b5)

time: 896 us -> 865 us (0.965)
  local copies, waits for them, and re-layouts: 117 us -> 97.3 us
  waiting for transfers between devices: 197 us -> 215 us
  other arithmetic: 157 us -> 142 us
  matrix products: 140 us -> 127 us
    ppermute x69 -> x71, waiting for transfers between devices: 149 us -> 166 us  [swap(): return lax.ppermute(values, axis_name, [(i, i ^ bit) for i in range(size)])]
    dot_general x4, matrix products: 36.6 us -> 27 us  [times(): jnp.einsum('slk,kn->sln', values, matrix, preferred_element_type=dtype)]
    slice x22 -> x24, local copies, waits for them, and re-layouts: 29.5 us -> 24.2 us  [lane_blocks(): runs.append(values[:, wanted[start] * width:(wanted[stop - 1] + 1) * width])]
    convert_element_type x22 -> x24, other arithmetic: 44.7 us -> 39.5 us  [shrink(): (keep.astype(F32) + swap(send, 'fsdp', 2 * bit).astype(F32)).astype(BF)]
    unnamed x180 -> x214, local copies, waits for them, and re-layouts: 28.7 us -> 24.7 us
    ppermute x69 -> x71, starting transfers between devices: 58.3 us -> 57.7 us  [swap(): return lax.ppermute(values, axis_name, [(i, i ^ bit) for i in range(size)])]
  transfers between devices with their start and end apart: 85 -> 87, of which waited for: 38 -> 41; matrix products, arithmetic and copies ran while one was open for 39% -> 35% of each run, Pallas kernels for 19% -> 20%
where the time goes in v3:
time: 865 us; the launch traced here: 853 us
  waiting for transfers between devices  215 us (25%)
  Pallas kernels  175 us (20%)
  other arithmetic  142 us (16%)
  matrix products  127 us (15%)
  local copies, waits for them, and re-layouts  97.3 us (11%)
  starting transfers between devices  77.2 us (9%)
  between operations  20.1 us (2%)
    ppermute x71, waiting for transfers between devices, swap(): return lax.ppermute(values, axis_name, [(i, i ^ bit) for i in range(size)])  166 us
    dot_general x6, matrix products, times_t(): jnp.einsum('sln,kn->slk', values, matrix, preferred_element_type=dtype)  70.2 us
    ppermute x71, starting transfers between devices, swap(): return lax.ppermute(values, axis_name, [(i, i ^ bit) for i in range(size)])  57.7 us
    convert_element_type x24, other arithmetic, shrink(): (keep.astype(F32) + swap(send, 'fsdp', 2 * bit).astype(F32)).astype(BF)  39.5 us
    pallas_call x1, Pallas kernels, run_backward_gates(): pl.pallas_call(backward_gates_kernel, grid=(channels // width, seqs), in_...  38.1 us
    all_gather x4, waiting for transfers between devices, all_z(): return lax.all_gather(values, 'tp', axis=0, tiled=False)  35.8 us
    pallas_call x6, Pallas kernels, join(): pl.pallas_call(functools.partial(join_kernel, half, [len(g) for g in grou...  30.9 us
    dot_general x4, matrix products, outer_sum(): jnp.einsum('slk,sln->kn', values, cotangent, preferred_element_type=F32)  29.9 us
  transfers between devices with their start and end apart: 87, of which 41 were waited for; matrix products, arithmetic and copies ran while one was open for 35% of the time, Pallas kernels for 20%

profile of v3, /device:TPU:0, one launch (start us, length us, event | category | flops | bytes accessed | tf_op | source)
XLA Modules:
  0.0 853.0 jit_solution(16608971150573235228)
XLA Ops:
  30.8 29.6 %all-gather.9.cloned.1.call-done = bf16[2432,384]{1,0:T(8,128)(2,1)} async-done(((bf16[608,384]{1,0:T(8,128)(2,1)}), bf16[2432,384]{1,0:T(8,128)(2,1)}) %all-gather.9.cloned.1.call-update) | async-done | bytes 1867792 | tf_op jit(solution)/shard_map/all_gather | solution.py:691
  92.5 14.3 %collective-permute-done.13.refs_2_ = bf16[1024,384]{1,0:T(8,128)(2,1)} collective-permute-done((bf16[1024,384]{1,0:T(8,128)(2,1)}, bf16[1024,384]{1,0:T(8,128)(2,1)}, u32[]{:S(2)}, u32[]{:S(2)}) %collective-permute-start.13) | collective-permute-done | bytes 786464 | tf_op jit(solution)/shard_map/ppermute | solution.py:22
  188.4 27.5 %forward_scan.1 = (bf16[4,256,1024]{2,1,0:T(8,128)(2,1)}, f32[4,256,1024]{2,1,0:T(8,128)}, f32[4,256,1024]{2,1,0:T(8,128)}, f32[4,256,1024]{2,1,0:T(8,128)}) custom-call(f32[4,256,1024]{2,1,0:T(8,128)} %copy-done.13, f32[4,8,1024]{2,1,0:T(8,128)} %pad.20.halo, f32[4,1024]{1,0:T(4,128)} %slice.540.conv_w, f32[4,1024]{1,0:T(4,128)} %pad_maximum_fusion.33.vectors, ...), custom_call_target="tpu_custom_call" | custom-call | flops 1 | bytes 1 | tf_op jit(solution)/shard_map/forward_scan/pallas_call | solution.py:239
  225.5 8.0 collective-permute-start.19
  240.0 14.0 %fusion.35 = (bf16[4,256,1024]{2,1,0:T(8,128)(2,1)}, f32[4,256,1024]{2,1,0:T(8,128)}, f32[4,256,1024]{2,1,0:T(8,128)}) fusion(f32[4,256,1024]{2,1,0:T(8,128)} %get-tuple-element.200, f32[4,256,1024]{2,1,0:T(8,128)} %get-tuple-element.201, f32[4,1024]{1,0:T(4,128)S(1)} %bitcast.291, f32[1024]{0:T(1024)S(1)} %bitcast.294, ...), kind=kOutput, calls=%fused_computation.55 | convolution fusion | flops 3234856960 | bytes 25186304 | tf_op jit(solution)/shard_map/sln,kn->slk/dot_general | solution.py:601
  254.0 7.6 fusion.39
  261.6 12.5 %collective-permute-done.26.refs_3_ = bf16[2304,384]{1,0:T(8,128)(2,1)} collective-permute-done((bf16[2304,384]{1,0:T(8,128)(2,1)}, bf16[2304,384]{1,0:T(8,128)(2,1)}, u32[]{:S(2)}, u32[]{:S(2)}) %collective-permute-start.26) | collective-permute-done | bytes 1769504 | tf_op jit(solution)/shard_map/ppermute | solution.py:22
  304.3 9.9 %fusion.24 = f32[4,256,2304]{2,1,0:T(8,128)} fusion(bf16[4,256,1536]{2,1,0:T(8,128)(2,1)S(1)} %multiply_convert_fusion.1, bf16[2304,1536]{1,0:T(8,128)(2,1)S(1)} %copy-done.3), kind=kOutput, calls=%fused_computation.32 | convolution fusion | flops 7247757312 | bytes 19660800 | tf_op jit(solution)/shard_map/sln,kn->slk/dot_general | solution.py:601
  314.2 16.5 %fusion.8 = (bf16[4,256,2304]{2,1,0:T(8,128)(2,1)}, f32[4,256,2304]{2,1,0:T(8,128)}) fusion(f32[4,256,2304]{2,1,0:T(8,128)} %fusion.24, bf16[4,256,1536]{2,1,0:T(8,128)(2,1)S(1)} %multiply_convert_fusion.1, bf16[2304,1536]{1,0:T(8,128)(2,1)} %join.10.second_w), kind=kOutput, calls=%fused_computation.12 | convolution fusion | flops 7271350272 | bytes 33816576 | tf_op jit(solution)/shard_map/sln,kn->slk/dot_general | solution.py:601
  331.2 9.8 %collective-permute-done.32.refs_3_ = bf16[1152,384]{1,0:T(8,128)(2,1)} collective-permute-done((bf16[1152,384]{1,0:T(8,128)(2,1)}, bf16[1152,384]{1,0:T(8,128)(2,1)}, u32[]{:S(2)}, u32[]{:S(2)}) %collective-permute-start.32) | collective-permute-done | bytes 884768 | tf_op jit(solution)/shard_map/ppermute | solution.py:22
  350.1 12.3 %fusion.20 = bf16[4,256,1536]{2,1,0:T(8,128)(2,1)} fusion(bf16[4,256,2304]{2,1,0:T(8,128)(2,1)} %get-tuple-element.238, bf16[2304,1536]{1,0:T(8,128)(2,1)} %join.11), kind=kOutput, calls=%fused_computation.28 | convolution fusion | flops 7247757312 | bytes 14942208 | tf_op jit(solution)/shard_map/slk,kn->sln/dot_general | solution.py:597
  379.2 9.4 %bitcast_convert_fusion = bf16[2304,1536]{1,0:T(8,128)(2,1)} fusion(bf16[4,256,2304]{2,1,0:T(8,128)(2,1)S(1)} %bitcast.311, bf16[4,256,1536]{2,1,0:T(8,128)(2,1)S(1)} %get-tuple-element.250), kind=kOutput, calls=%fused_computation | convolution fusion | flops 7251296256 | bytes 14942208 | tf_op jit(solution)/shard_map/slk,sln->kn/dot_general | solution.py:605
  388.7 18.2 %multiply_convert_fusion = (bf16[4,256,2304]{2,1,0:T(8,128)(2,1)}, bf16[4,256,2304]{2,1,0:T(8,128)(2,1)}) fusion(f32[4,256,2304]{2,1,0:T(8,128)} %fusion.24, f32[4,256,2304]{2,1,0:T(8,128)} %get-tuple-element.539, bf16[4,256,1536]{2,1,0:T(8,128)(2,1)S(1)} %get-tuple-element.250, bf16[2304,1536]{1,0:T(8,128)(2,1)} %join.11), kind=kOutput, calls=%fused_computation.22 | convolution fusion | flops 7299661824 | bytes 38535168 | tf_op jit(solution)/shard_map/sln,kn->slk/dot_general | solution.py:601
  406.9 13.4 %outer.2 = bf16[2304,1536]{1,0:T(8,128)(2,1)} custom-call(bf16[1024,2304]{1,0:T(8,128)(2,1)} %bitcast.229, bf16[1024,1536]{1,0:T(8,128)(2,1)} %bitcast.224), custom_call_target="tpu_custom_call" | custom-call | flops 1 | bytes 1 | tf_op jit(solution)/shard_map/outer/pallas_call | solution.py:498
  429.2 13.4 %outer.3 = bf16[2304,1536]{1,0:T(8,128)(2,1)} custom-call(bf16[1024,2304]{1,0:T(8,128)(2,1)} %bitcast.227, bf16[1024,1536]{1,0:T(8,128)(2,1)} %bitcast.225), custom_call_target="tpu_custom_call" | custom-call | flops 1 | bytes 1 | tf_op jit(solution)/shard_map/outer/pallas_call | solution.py:498
  442.5 21.0 %two_products.1 = bf16[1024,1536]{1,0:T(8,128)(2,1)} custom-call(bf16[1024,2304]{1,0:T(8,128)(2,1)} %bitcast.230, bf16[2304,1536]{1,0:T(8,128)(2,1)} %join.9.first_w, bf16[1024,2304]{1,0:T(8,128)(2,1)} %bitcast.228, bf16[2304,1536]{1,0:T(8,128)(2,1)} %join.10.second_w), custom_call_target="tpu_custom_call" | custom-call | flops 1 | bytes 1 | tf_op jit(solution)/shard_map/two_products/pallas_call | solution.py:526
  495.2 28.2 %collective-permute-done.42 = bf16[1152,768]{1,0:T(8,128)(2,1)} collective-permute-done((bf16[1152,768]{1,0:T(8,128)(2,1)}, bf16[1152,768]{1,0:T(8,128)(2,1)}, u32[]{:S(2)}, u32[]{:S(2)}) %collective-permute-start.42) | collective-permute-done | bytes 1769504 | tf_op jit(solution)/shard_map/ppermute | solution.py:22
  525.8 12.7 %norm_back.1 = (f32[1024,1536]{1,0:T(8,128)}, bf16[1024,1536]{1,0:T(8,128)(2,1)}, f32[8,1536]{1,0:T(8,128)}) custom-call(f32[1024,1536]{1,0:T(8,128)} %bitcast.221, f32[1,1536]{1,0:T(1,128)} %broadcast_in_dim.7.gain, bf16[1024,1536]{1,0:T(8,128)(2,1)} %bitcast.49.mine, bf16[1024,1536]{1,0:T(8,128)(2,1)} %bitcast.50.other, f32[1024,1536]{1,0:T(8,128)} %bitcast.226), custom_call_target="tpu_custom_call" | custom-call | flops 1 | bytes 1 | tf_op jit(solution)/shard_map/norm_back/pallas_call | solution.py:567
  553.6 17.8 %backward_scan.1 = (bf16[4,256,1024]{2,1,0:T(8,128)(2,1)}, f32[4,256,1024]{2,1,0:T(8,128)}, f32[4,256,1024]{2,1,0:T(8,128)}) custom-call(f32[4,256,1024]{2,1,0:T(8,128)} %fusion.37.d_mixed, f32[4,256,1024]{2,1,0:T(8,128)} %get-tuple-element.537.gate_pre, f32[4,256,1024]{2,1,0:T(8,128)} %get-tuple-element.396.state, f32[4,256,1024]{2,1,0:T(8,128)} %get-tuple-element.260.decay), custom_call_target="tpu_custom_call" | custom-call | flops 1 | bytes 1 | tf_op jit(solution)/shard_map/backward_scan/pallas_call | solution.py:307
  576.3 7.8 bitcast_convert_fusion.3
  603.4 11.0 %collective-permute-done.46 = bf16[1152,384]{1,0:T(8,128)(2,1)S(1)} collective-permute-done((bf16[1152,384]{1,0:T(8,128)(2,1)S(1)}, bf16[1152,384]{1,0:T(8,128)(2,1)S(1)}, u32[]{:S(2)}, u32[]{:S(2)}) %collective-permute-start.46) | collective-permute-done | bytes 884768 | tf_op jit(solution)/shard_map/ppermute | solution.py:22
  650.6 38.1 %backward_gates.1 = (bf16[4,256,1024]{2,1,0:T(8,128)(2,1)}, f32[4,8,1024]{2,1,0:T(8,128)}, f32[4,8,1024]{2,1,0:T(8,128)}, f32[4,256,256]{2,1,0:T(8,128)}, f32[4,256,256]{2,1,0:T(8,128)}, /*index=5*/f32[8,8,1024]{2,1,0:T(8,128)}) custom-call(f32[4,256,1024]{2,1,0:T(8,128)} %get-tuple-element.274.local_c, f32[4,256,1024]{2,1,0:T(8,128)} %get-tuple-element.275.prod_c, ...), custom_call_target="tpu_custom_call" | custom-call | flops 1 | bytes 1 | tf_op jit(solution)/shard_map/backward_gates/pallas_call | solution.py:439
  710.1 7.7 bitcast_convert_fusion.1
  744.4 9.6 %collective-permute-done.58 = bf16[512,768]{1,0:T(8,128)(2,1)} collective-permute-done((bf16[512,768]{1,0:T(8,128)(2,1)}, bf16[512,768]{1,0:T(8,128)(2,1)}, u32[]{:S(2)}, u32[]{:S(2)}) %collective-permute-start.58) | collective-permute-done | bytes 786464 | tf_op jit(solution)/shard_map/ppermute | solution.py:22
  (642 shorter events, 462.6 us)
Async XLA Ops:
  7.2 53.2 %all-gather.9.cloned.1.call-start = ((), (), s32[]{:S(2)}) async-start(), calls=%async_computation.8 | async-start | bytes 2334720 | tf_op jit(solution)/shard_map/all_gather | solution.py:691
  16.0 116.7 %all-gather.11.cloned.1.call-start = ((), (), s32[]{:S(2)}) async-start(), calls=%async_computation.9 | async-start | bytes 4423680 | tf_op jit(solution)/shard_map/all_gather | solution.py:691
  23.1 52.7 %collective-permute-start.2 = (bf16[2,256,1536]{2,1,0:T(8,128)(2,1)S(1)}, bf16[2,256,1536]{2,1,0:T(8,128)(2,1)}, u32[]{:S(2)}, u32[]{:S(2)}) collective-permute-start(bf16[2,256,1536]{2,1,0:T(8,128)(2,1)S(1)} %copy-done.45), channel_id=1, source_target_pairs={{0,4},{4,0},{8,12},{12,8},{16,20},{20,16},{24,28},{28,24},{1,5},{5... | collective-permute-start | bytes 4718600 | tf_op jit(solution)/shard_map/ppermute | solution.py:22
  60.4 193.5 %all-gather.13.cloned.1.call-start = ((), (), s32[]{:S(2)}) async-start(), calls=%async_computation.10 | async-start | bytes 3932160 | tf_op jit(solution)/shard_map/all_gather | solution.py:691
  87.0 49.9 %collective-permute-start.10 = (bf16[1408,384]{1,0:T(8,128)(2,1)}, bf16[1408,384]{1,0:T(8,128)(2,1)}, u32[]{:S(2)}, u32[]{:S(2)}) collective-permute-start(bf16[1408,384]{1,0:T(8,128)(2,1)} %pad_maximum_fusion.13.refs_0_), channel_id=1, source_target_pairs={{0,16},{4,20},{8,24},{12,28},{16,0},{20,4},{24,8},{28,12},{1,17},{... | collective-permute-start | bytes 3244040 | tf_op jit(solution)/shard_map/ppermute | solution.py:22
  88.2 48.7 %collective-permute-start.12 = (bf16[1024,384]{1,0:T(8,128)(2,1)}, bf16[1024,384]{1,0:T(8,128)(2,1)}, u32[]{:S(2)}, u32[]{:S(2)}) collective-permute-start(bf16[1024,384]{1,0:T(8,128)(2,1)} %bitcast.10.refs_0_), channel_id=1, source_target_pairs={{0,8},{4,12},{8,0},{12,4},{16,24},{20,28},{24,16},{28,20},{1,9},{5... | collective-permute-start | bytes 2359304 | tf_op jit(solution)/shard_map/ppermute | solution.py:22
  149.1 112.5 %all-gather.15.cloned.1.call-start = ((), (), s32[]{:S(2)}) async-start(), calls=%async_computation.11 | async-start | bytes 2211840 | tf_op jit(solution)/shard_map/all_gather | solution.py:691
  151.1 425.2 %reduce-scatter.5.cloned.1.call-start = ((), (), s32[]{:S(2)}) async-start(), calls=%async_computation.4 | async-start | bytes 8847360 | tf_op jit(solution)/shard_map/reduce_scatter | solution.py:823
  160.7 76.1 %collective-permute-start.22 = (bf16[2304,384]{1,0:T(8,128)(2,1)}, bf16[2304,384]{1,0:T(8,128)(2,1)}, u32[]{:S(2)}, u32[]{:S(2)}) collective-permute-start(bf16[2304,384]{1,0:T(8,128)(2,1)} %bitcast.235), channel_id=1, source_target_pairs={{0,8},{4,12},{8,0},{12,4},{16,24},{20,28},{24,16},{28,20},{1,9},{5... | collective-permute-start | bytes 5308424 | tf_op jit(solution)/shard_map/ppermute | solution.py:22
  161.8 76.6 %collective-permute-start.24 = (bf16[2304,384]{1,0:T(8,128)(2,1)}, bf16[2304,384]{1,0:T(8,128)(2,1)}, u32[]{:S(2)}, u32[]{:S(2)}) collective-permute-start(bf16[2304,384]{1,0:T(8,128)(2,1)} %bitcast.236), channel_id=1, source_target_pairs={{0,16},{4,20},{8,24},{12,28},{16,0},{20,4},{24,8},{28,12},{1,17},{... | collective-permute-start | bytes 5308424 | tf_op jit(solution)/shard_map/ppermute | solution.py:22
  162.4 76.0 %collective-permute-start.23 = (bf16[2304,384]{1,0:T(8,128)(2,1)}, bf16[2304,384]{1,0:T(8,128)(2,1)}, u32[]{:S(2)}, u32[]{:S(2)}) collective-permute-start(bf16[2304,384]{1,0:T(8,128)(2,1)} %bitcast.232), channel_id=1, source_target_pairs={{0,16},{4,20},{8,24},{12,28},{16,0},{20,4},{24,8},{28,12},{1,17},{... | collective-permute-start | bytes 5308424 | tf_op jit(solution)/shard_map/ppermute | solution.py:22
  163.9 74.6 %collective-permute-start.25 = (bf16[2304,384]{1,0:T(8,128)(2,1)}, bf16[2304,384]{1,0:T(8,128)(2,1)}, u32[]{:S(2)}, u32[]{:S(2)}) collective-permute-start(bf16[2304,384]{1,0:T(8,128)(2,1)} %bitcast.233), channel_id=1, source_target_pairs={{0,8},{4,12},{8,0},{12,4},{16,24},{20,28},{24,16},{28,20},{1,9},{5... | collective-permute-start | bytes 5308424 | tf_op jit(solution)/shard_map/ppermute | solution.py:22
  388.6 338.5 %reduce-scatter.7.cloned.1.call-start = ((), (), s32[]{:S(2)}) async-start(), calls=%async_computation.5 | async-start | bytes 4423680 | tf_op jit(solution)/shard_map/reduce_scatter | solution.py:857
  424.1 40.9 %collective-permute-start.38 = (bf16[1152,768]{1,0:T(8,128)(2,1)}, bf16[1152,768]{1,0:T(8,128)(2,1)}, u32[]{:S(2)}, u32[]{:S(2)}) collective-permute-start(bf16[1152,768]{1,0:T(8,128)(2,1)} %pad_maximum_fusion.6), channel_id=1, source_target_pairs={{0,8},{4,12},{8,0},{12,4},{16,24},{20,28},{24,16},{28,20},{1,9},{5... | collective-permute-start | bytes 5308424 | tf_op jit(solution)/shard_map/ppermute | solution.py:22
  426.9 41.3 %collective-permute-start.37 = (bf16[1152,768]{1,0:T(8,128)(2,1)S(1)}, bf16[1152,768]{1,0:T(8,128)(2,1)}, u32[]{:S(2)}, u32[]{:S(2)}) collective-permute-start(bf16[1152,768]{1,0:T(8,128)(2,1)S(1)} %slice.566), channel_id=1, source_target_pairs={{0,16},{4,20},{8,24},{12,28},{16,0},{20,4},{24,8},{28,12},{1,17},{... | collective-permute-start | bytes 5308424 | tf_op jit(solution)/shard_map/ppermute | solution.py:22
  471.9 53.9 %collective-permute-start.39 = (bf16[4,256,1536]{2,1,0:T(8,128)(2,1)}, bf16[4,256,1536]{2,1,0:T(8,128)(2,1)}, u32[]{:S(2)}, u32[]{:S(2)}) collective-permute-start(bf16[4,256,1536]{2,1,0:T(8,128)(2,1)} %bitcast.48), channel_id=1, source_target_pairs={{0,4},{4,0},{8,12},{12,8},{16,20},{20,16},{24,28},{28,24},{1,5},{5... | collective-permute-start | bytes 9437192 | tf_op jit(solution)/shard_map/ppermute | solution.py:22
  482.1 41.3 %collective-permute-start.42 = (bf16[1152,768]{1,0:T(8,128)(2,1)}, bf16[1152,768]{1,0:T(8,128)(2,1)}, u32[]{:S(2)}, u32[]{:S(2)}) collective-permute-start(bf16[1152,768]{1,0:T(8,128)(2,1)} %slice.576), channel_id=1, source_target_pairs={{0,16},{4,20},{8,24},{12,28},{16,0},{20,4},{24,8},{28,12},{1,17},{... | collective-permute-start | bytes 5308424 | tf_op jit(solution)/shard_map/ppermute | solution.py:22
  486.7 55.3 %collective-permute-start.43 = (bf16[1152,768]{1,0:T(8,128)(2,1)}, bf16[1152,768]{1,0:T(8,128)(2,1)}, u32[]{:S(2)}, u32[]{:S(2)}) collective-permute-start(bf16[1152,768]{1,0:T(8,128)(2,1)} %pad_maximum_fusion.7), channel_id=1, source_target_pairs={{0,8},{4,12},{8,0},{12,4},{16,24},{20,28},{24,16},{28,20},{1,9},{5... | collective-permute-start | bytes 5308424 | tf_op jit(solution)/shard_map/ppermute | solution.py:22
  622.8 164.6 %reduce-scatter.9.cloned.1.call-start = ((), (), s32[]{:S(2)}) async-start(), calls=%async_computation.6 | async-start | bytes 1966080 | tf_op jit(solution)/shard_map/reduce_scatter | solution.py:800
  633.8 59.3 %collective-permute-start.52 = (bf16[1024,768]{1,0:T(8,128)(2,1)}, bf16[1024,768]{1,0:T(8,128)(2,1)}, u32[]{:S(2)}, u32[]{:S(2)}) collective-permute-start(bf16[1024,768]{1,0:T(8,128)(2,1)} %pad_maximum_fusion.11), channel_id=1, source_target_pairs={{0,8},{4,12},{8,0},{12,4},{16,24},{20,28},{24,16},{28,20},{1,9},{5... | collective-permute-start | bytes 4718600 | tf_op jit(solution)/shard_map/ppermute | solution.py:22
  636.8 58.1 %collective-permute-start.51 = (bf16[1024,768]{1,0:T(8,128)(2,1)}, bf16[1024,768]{1,0:T(8,128)(2,1)}, u32[]{:S(2)}, u32[]{:S(2)}) collective-permute-start(bf16[1024,768]{1,0:T(8,128)(2,1)} %slice.601), channel_id=1, source_target_pairs={{0,16},{4,20},{8,24},{12,28},{16,0},{20,4},{24,8},{28,12},{1,17},{... | collective-permute-start | bytes 4718600 | tf_op jit(solution)/shard_map/ppermute | solution.py:22
  647.4 45.6 %collective-permute-start.53 = (bf16[288,384]{1,0:T(8,128)(2,1)S(1)}, bf16[288,384]{1,0:T(8,128)(2,1)S(1)}, u32[]{:S(2)}, u32[]{:S(2)}) collective-permute-start(bf16[288,384]{1,0:T(8,128)(2,1)S(1)} %slice.607), channel_id=1, source_target_pairs={{0,8},{4,12},{8,0},{12,4},{16,24},{20,28},{24,16},{28,20},{1,9},{5... | collective-permute-start | bytes 663560 | tf_op jit(solution)/shard_map/ppermute | solution.py:22
  648.8 44.3 %collective-permute-start.54 = (bf16[288,384]{1,0:T(8,128)(2,1)S(1)}, bf16[288,384]{1,0:T(8,128)(2,1)S(1)}, u32[]{:S(2)}, u32[]{:S(2)}) collective-permute-start(bf16[288,384]{1,0:T(8,128)(2,1)S(1)} %slice.609), channel_id=1, source_target_pairs={{0,16},{4,20},{8,24},{12,28},{16,0},{20,4},{24,8},{28,12},{1,17},{... | collective-permute-start | bytes 663560 | tf_op jit(solution)/shard_map/ppermute | solution.py:22
  739.9 99.8 %reduce-scatter.11.cloned.1.call-start = ((), (), s32[]{:S(2)}) async-start(), calls=%async_computation.7 | async-start | bytes 1351680 | tf_op jit(solution)/shard_map/reduce_scatter | solution.py:903
  (155 other events, 2375.1 us)
Sparse Core Ops, SparseCore 0:
  16.1 44.2 all-gather.8
  62.5 70.0 all-gather.10
  149.2 60.9 all-gather.12
  212.2 40.0 all-gather.14
  388.7 122.4 reduce-scatter.4
  622.9 67.2 reduce-scatter.6
  740.0 37.0 reduce-scatter.8
  804.5 30.9 reduce-scatter.10
